TPU v7x, 16 devices: a 4x2x1 block of a 4x4x8 slice. The times are simulated.
16 devices in a mesh: ens: 2 (over y, z), feat: 8 (over x, core).
Axes of the slice: x: 4, y: 2, z: 1, core: 2. Of those that a mesh axis runs over, the one named last changes fastest.
The devices are a block of a 4x4x8 slice.
Arguments:
- particles: float32 [1024, 32768], P('ens', 'feat'), parts along dimension 0
- prec_diag: float32 [65536], P(('ens', 'feat')), parts along dimension 0
- low_factor: bfloat16 [65536, 32], P(('ens', 'feat')), parts along dimension 0
- prior_mean: float32 [65536], P(('ens', 'feat')), parts along dimension 0
- data_mat: bfloat16 [2048, 32768], P('ens', 'feat'), parts along dimension 0
- labels: int32 [2048], P('ens'), parts along dimension 0
Outputs:
- output: float32 [1024, 32768], P('ens', 'feat'), parts along dimension 0
There are 2 independent parts. A program takes and returns all parts, laid end to end along the dimension named above; each array names one.
All inputs are finite; a program needn't handle non-finite values.
Results may differ from a plain program's by a relative error of at most 0.001.
Values are sent between devices in bfloat16 or wider.
A program may use at most 768 MiB of HBM per device.

v0:
```python
import math
import jax
import jax.numpy as jnp
from jax import lax
from jax.sharding import PartitionSpec as P

NUM_STEPS = 3
DIMS_NT = (((1,), (1,)), ((), ()))


def solution(mesh):
    feat_size = mesh.shape["feat"]

    def local_run(particles, prec_diag, low_factor, prior_mean, data_mat, labels):
        n_part, dim_local = particles.shape
        dim_full = dim_local * feat_size
        m_rows = data_mat.shape[0]
        band_width = 2.0 * dim_full
        step_size = dim_full / 4.0
        lik_weight = 2.0 / math.sqrt(m_rows * dim_full)
        targets = labels.astype(jnp.float32)[None, :]
        state = particles
        for step_idx in range(NUM_STEPS):
            part_bf = state.astype(jnp.bfloat16)
            centred = state - prior_mean
            projected = lax.psum(jnp.dot(centred.astype(jnp.bfloat16), low_factor, preferred_element_type=jnp.float32), "feat")
            gram_mat = lax.psum(lax.dot_general(part_bf, part_bf, DIMS_NT, preferred_element_type=jnp.float32), "feat")
            logits = lax.psum(lax.dot_general(part_bf, data_mat, DIMS_NT, preferred_element_type=jnp.float32), "feat")
            sq_norm = jnp.diagonal(gram_mat)
            sq_dist = jnp.maximum(sq_norm[:, None] + sq_norm[None, :] - 2.0 * gram_mat, 0.0)
            kernel = jnp.exp(-sq_dist / band_width)
            residual = targets - jax.nn.sigmoid(logits)
            low_rank = lax.dot_general(projected.astype(jnp.bfloat16), low_factor, DIMS_NT, preferred_element_type=jnp.float32)
            lik_term = jnp.dot(residual.astype(jnp.bfloat16), data_mat, preferred_element_type=jnp.float32)
            log_grad = lik_weight * lik_term - centred * prec_diag - low_rank
            kern_bf = kernel.astype(jnp.bfloat16)
            driving = jnp.dot(kern_bf, log_grad.astype(jnp.bfloat16), preferred_element_type=jnp.float32)
            pulled = jnp.dot(kern_bf, part_bf, preferred_element_type=jnp.float32)
            row_sum = jnp.sum(kernel, axis=1, keepdims=True)
            update_dir = (driving + (2.0 / band_width) * (row_sum * state - pulled)) / n_part
            state = state + step_size * update_dir
        return state

    return jax.shard_map(
        local_run,
        mesh=mesh,
        in_specs=(P("ens", "feat"), P(("ens", "feat")), P(("ens", "feat"), None),
                  P(("ens", "feat")), P("ens", "feat"), P("ens")),
        out_specs=P("ens", "feat"),
        check_vma=False,
    )
```

profile of v0, /device:TPU:113, one launch (start us, length us, event | category | flops | bytes accessed | tf_op | source)
XLA Modules:
  0.0 383.0 jit_solution(1448820220174277176)
XLA Ops:
  6.5 0.0 copy-start
  6.6 0.0 all-reduce.11.cloned.1.call-start
  6.6 0.0 copy-start.3
  6.6 9.3 %fusion.40 = f32[512,512]{1,0:T(8,128)} fusion(f32[512,4096]{1,0:T(8,128)} %param.6), kind=kOutput, calls=%fused_computation.59 | convolution fusion | flops 2149580800 | bytes 9437184 | tf_op jit(solution)/shard_map/dot_general | solution.py:27
  15.8 0.0 copy-done.3
  15.8 0.0 copy-start.9
  15.8 0.0 copy-start.7
  15.8 8.4 %fusion.38 = f32[512,1024]{1,0:T(8,128)} fusion(bf16[1024,4096]{1,0:T(8,128)(2,1)} %param.10, f32[512,4096]{1,0:T(8,128)S(1)} %copy-done.3), kind=kOutput, calls=%fused_computation.57 | convolution fusion | flops 4297064448 | bytes 18874368 | tf_op jit(solution)/shard_map/dot_general | solution.py:28
  24.2 0.1 all-reduce.11.cloned.1.call-update
  24.2 0.1 all-reduce.9.cloned.1.call-start
  24.3 0.0 copy-done.9
  24.3 0.0 copy-done
  24.3 0.0 copy-done.7
  24.3 4.6 %fusion = f32[512,32]{1,0:T(8,128)S(1)} fusion(bf16[4096,32]{0,1:T(8,128)(2,1)S(1)} %copy-done, f32[512,4096]{1,0:T(8,128)} %param.6, f32[4096]{0:T(1024)S(1)} %copy-done.7), kind=kOutput, calls=%fused_computation.12 | convolution fusion | flops 138412032 | bytes 8732672 | tf_op jit(solution)/shard_map/dot_general | solution.py:26
  29.0 27.8 %psum.65 = bf16[512,32]{1,0:T(8,128)(2,1)S(1)} all-reduce(f32[512,32]{1,0:T(8,128)S(1)} %fusion), channel_id=1, replica_groups=mesh['ens'=2,'feat'=8] {'feat'}, use_global_device_ids=true, to_apply=%region_2.0 | all-reduce | flops 16384 | bytes 98304 | tf_op jit(solution)/shard_map/psum | solution.py:26
  56.8 30.0 %all-reduce.11.cloned.1.call-done = (f32[512,512]{1,0:T(8,128)}, f32[512,1024]{1,0:T(8,128)}) async-done(((f32[512,512]{1,0:T(8,128)}, f32[512,1024]{1,0:T(8,128)}), (f32[512,512]{1,0:T(8,128)}, f32[512,1024]{1,0:T(8,128)})) %all-reduce.11.cloned.1.call-update) | async-done | bytes 3145744 | tf_op jit(solution)/shard_map/psum | solution.py:27
  86.8 8.6 %gather_fusion = f32[512]{0:T(512)S(1)} fusion(f32[512,512]{1,0:T(8,128)} %get-tuple-element.9, s32[512]{0:T(512)S(1)} %bitcast.16), kind=kCustom, calls=%fused_computation | custom fusion | bytes 8192 | tf_op jit(solution)/shard_map/jit(diagonal)/cond/branch_0_fun/gather | solution.py:29
  95.4 1.7 fusion.15
  97.1 0.0 copy-start.4
  97.1 0.0 copy-start.8
  97.1 12.0 %fusion.6 = f32[512,4096]{1,0:T(8,128)} fusion(bf16[1024,4096]{1,0:T(8,128)(2,1)} %param.10, f32[512,1024]{1,0:T(8,128)} %get-tuple-element.10, f32[1024]{0:T(1024)S(1)} %convert_element_type.59), kind=kOutput, calls=%fused_computation.21 | convolution fusion | flops 4297588736 | bytes 18878464 | tf_op jit(solution)/shard_map/dot_general | solution.py:34
  109.1 0.0 copy-done.4
  109.1 0.0 copy-done.8
  109.1 13.2 %fusion.53 = f32[512,4096]{1,0:T(8,128)} fusion(f32[512,512]{1,0:T(8,128)S(1)} %copy-done.4, f32[512]{0:T(512)S(1)} %gather_fusion, f32[512,4096]{1,0:T(8,128)} %fusion.6, f32[512,4096]{1,0:T(8,128)} %param.6, bf16[4096,32]{0,1:T(8,128)(2,1)S(1)} %copy-done, f32[4096]{0:T(1024)S(1)} %copy-done.8, f32[4096]{0:T(1024)S(1)} %copy-done.7, ...), kind=kOutput, calls=%fused_computation.63 | convolution fusion | flops 2296119296 | bytes 26544128 | tf_op jit(solution)/shard_map/dot_general | solution.py:37
  122.3 12.1 %multiply_add_fusion.2 = f32[512,4096]{1,0:T(8,128)S(1)} fusion(f32[512,4096]{1,0:T(8,128)} %param.6, f32[512,4096]{1,0:T(8,128)} %fusion.53, f32[512]{0:T(512)S(1)} %fusion.15, f32[512,512]{1,0:T(8,128)S(1)} %copy-done.4, f32[512]{0:T(512)S(1)} %gather_fusion), kind=kOutput, calls=%fused_computation.7 | convolution fusion | flops 2163998720 | bytes 26218496 | tf_op jit(solution)/shard_map/dot_general | solution.py:38
  134.4 0.0 copy-start.2
  134.4 3.7 fusion.32
  138.2 0.0 copy-done.2
  138.2 8.5 %fusion.30 = f32[512,1024]{1,0:T(8,128)} fusion(bf16[1024,4096]{1,0:T(8,128)(2,1)} %param.10, f32[512,4096]{1,0:T(8,128)S(1)} %multiply_add_fusion.2), kind=kOutput, calls=%fused_computation.49 | convolution fusion | flops 4297064448 | bytes 18874368 | tf_op jit(solution)/shard_map/dot_general | solution.py:28
  146.7 0.1 all-reduce.9.cloned.1.call-update
  146.8 0.1 all-reduce.7.cloned.1.call-start
  146.8 4.6 %fusion.1 = f32[512,32]{1,0:T(8,128)S(1)} fusion(bf16[4096,32]{0,1:T(8,128)(2,1)S(1)} %copy-done, f32[512,4096]{1,0:T(8,128)} %copy-done.2, f32[4096]{0:T(1024)S(1)} %copy-done.7), kind=kOutput, calls=%fused_computation.13 | convolution fusion | flops 138412032 | bytes 8732672 | tf_op jit(solution)/shard_map/dot_general | solution.py:26
  151.4 27.9 %psum.68 = bf16[512,32]{1,0:T(8,128)(2,1)S(1)} all-reduce(f32[512,32]{1,0:T(8,128)S(1)} %fusion.1), channel_id=1, replica_groups=mesh['ens'=2,'feat'=8] {'feat'}, use_global_device_ids=true, to_apply=%region_6.7 | all-reduce | flops 16384 | bytes 98304 | tf_op jit(solution)/shard_map/psum | solution.py:26
  179.4 28.7 %all-reduce.9.cloned.1.call-done = (f32[512,512]{1,0:T(8,128)}, f32[512,1024]{1,0:T(8,128)}) async-done(((f32[512,512]{1,0:T(8,128)}, f32[512,1024]{1,0:T(8,128)}), (f32[512,512]{1,0:T(8,128)}, f32[512,1024]{1,0:T(8,128)})) %all-reduce.9.cloned.1.call-update) | async-done | bytes 3145744 | tf_op jit(solution)/shard_map/psum | solution.py:27
  208.1 8.7 %gather_fusion.1 = f32[512]{0:T(512)S(1)} fusion(f32[512,512]{1,0:T(8,128)} %get-tuple-element.7, s32[512]{0:T(512)S(1)} %bitcast.17), kind=kCustom, calls=%fused_computation.1 | custom fusion | bytes 8192 | tf_op jit(solution)/shard_map/jit(diagonal)/cond/branch_0_fun/gather | solution.py:29
  216.8 0.0 copy-start.5
  216.8 11.9 %fusion.7 = f32[512,4096]{1,0:T(8,128)} fusion(bf16[1024,4096]{1,0:T(8,128)(2,1)} %param.10, f32[512,1024]{1,0:T(8,128)} %get-tuple-element.8, f32[1024]{0:T(1024)S(1)} %convert_element_type.59), kind=kOutput, calls=%fused_computation.22 | convolution fusion | flops 4297588736 | bytes 18878464 | tf_op jit(solution)/shard_map/dot_general | solution.py:34
  228.7 0.0 copy-done.5
  228.7 0.5 fusion.17
  229.1 13.2 %fusion.48 = f32[512,4096]{1,0:T(8,128)} fusion(f32[512,512]{1,0:T(8,128)S(1)} %copy-done.5, f32[512]{0:T(512)S(1)} %gather_fusion.1, f32[512,4096]{1,0:T(8,128)} %fusion.7, f32[512,4096]{1,0:T(8,128)} %copy-done.2, bf16[4096,32]{0,1:T(8,128)(2,1)S(1)} %copy-done, f32[4096]{0:T(1024)S(1)} %copy-done.8, f32[4096]{0:T(1024)S(1)} %copy-done.7, ...), kind=kOutput, calls=%fused_computation.62 | convolution fusion | flops 2296119296 | bytes 26544128 | tf_op jit(solution)/shard_map/dot_general | solution.py:37
  242.3 12.2 %multiply_add_fusion.1 = f32[512,4096]{1,0:T(8,128)S(1)} fusion(f32[512,4096]{1,0:T(8,128)} %copy-done.2, f32[512,4096]{1,0:T(8,128)} %fusion.48, f32[512]{0:T(512)S(1)} %fusion.17, f32[512,512]{1,0:T(8,128)S(1)} %copy-done.5, f32[512]{0:T(512)S(1)} %gather_fusion.1), kind=kOutput, calls=%fused_computation.5 | convolution fusion | flops 2163998720 | bytes 26218496 | tf_op jit(solution)/shard_map/dot_general | solution.py:38
  254.5 0.0 copy-start.1
  254.5 3.6 fusion.27
  258.0 0.0 copy-done.1
  258.0 8.5 %fusion.25 = f32[512,1024]{1,0:T(8,128)} fusion(bf16[1024,4096]{1,0:T(8,128)(2,1)} %param.10, f32[512,4096]{1,0:T(8,128)S(1)} %multiply_add_fusion.1), kind=kOutput, calls=%fused_computation.44 | convolution fusion | flops 4297064448 | bytes 18874368 | tf_op jit(solution)/shard_map/dot_general | solution.py:28
  266.6 0.1 all-reduce.7.cloned.1.call-update
  266.6 4.6 %fusion.2 = f32[512,32]{1,0:T(8,128)S(1)} fusion(bf16[4096,32]{0,1:T(8,128)(2,1)S(1)} %copy-done, f32[512,4096]{1,0:T(8,128)} %copy-done.1, f32[4096]{0:T(1024)S(1)} %copy-done.7), kind=kOutput, calls=%fused_computation.14 | convolution fusion | flops 138412032 | bytes 8732672 | tf_op jit(solution)/shard_map/dot_general | solution.py:26
  271.2 27.9 %psum.71 = bf16[512,32]{1,0:T(8,128)(2,1)S(1)} all-reduce(f32[512,32]{1,0:T(8,128)S(1)} %fusion.2), channel_id=1, replica_groups=mesh['ens'=2,'feat'=8] {'feat'}, use_global_device_ids=true, to_apply=%region_10.11 | all-reduce | flops 16384 | bytes 98304 | tf_op jit(solution)/shard_map/psum | solution.py:26
  299.1 28.8 %all-reduce.7.cloned.1.call-done = (f32[512,512]{1,0:T(8,128)}, f32[512,1024]{1,0:T(8,128)}) async-done(((f32[512,512]{1,0:T(8,128)}, f32[512,1024]{1,0:T(8,128)}), (f32[512,512]{1,0:T(8,128)}, f32[512,1024]{1,0:T(8,128)})) %all-reduce.7.cloned.1.call-update) | async-done | bytes 3145744 | tf_op jit(solution)/shard_map/psum | solution.py:27
  327.9 8.7 %gather_fusion.2 = f32[512]{0:T(512)S(1)} fusion(f32[512,512]{1,0:T(8,128)} %get-tuple-element.5, s32[512]{0:T(512)S(1)} %bitcast.18), kind=kCustom, calls=%fused_computation.2 | custom fusion | bytes 8192 | tf_op jit(solution)/shard_map/jit(diagonal)/cond/branch_0_fun/gather | solution.py:29
  336.6 0.0 copy-start.6
  336.6 12.0 %fusion.8 = f32[512,4096]{1,0:T(8,128)} fusion(bf16[1024,4096]{1,0:T(8,128)(2,1)} %param.10, f32[512,1024]{1,0:T(8,128)} %get-tuple-element.6, f32[1024]{0:T(1024)S(1)} %convert_element_type.59), kind=kOutput, calls=%fused_computation.23 | convolution fusion | flops 4297588736 | bytes 18878464 | tf_op jit(solution)/shard_map/dot_general | solution.py:34
  348.6 0.0 copy-done.6
  348.6 0.5 fusion.19
  349.1 13.2 %fusion.43 = f32[512,4096]{1,0:T(8,128)} fusion(f32[512,512]{1,0:T(8,128)S(1)} %copy-done.6, f32[512]{0:T(512)S(1)} %gather_fusion.2, f32[512,4096]{1,0:T(8,128)} %fusion.8, f32[512,4096]{1,0:T(8,128)} %copy-done.1, bf16[4096,32]{0,1:T(8,128)(2,1)S(1)} %copy-done, f32[4096]{0:T(1024)S(1)} %copy-done.8, f32[4096]{0:T(1024)S(1)} %copy-done.7, ...), kind=kOutput, calls=%fused_computation.61 | convolution fusion | flops 2296119296 | bytes 26544128 | tf_op jit(solution)/shard_map/dot_general | solution.py:37
  362.2 14.0 %multiply_add_fusion = f32[512,4096]{1,0:T(8,128)} fusion(f32[512,4096]{1,0:T(8,128)} %copy-done.1, f32[512,4096]{1,0:T(8,128)} %fusion.43, f32[512]{0:T(512)S(1)} %fusion.19, f32[512,512]{1,0:T(8,128)S(1)} %copy-done.6, f32[512]{0:T(512)S(1)} %gather_fusion.2), kind=kOutput, calls=%fused_computation.3 | convolution fusion | flops 2163998720 | bytes 26218496 | tf_op jit(solution)/shard_map/dot_general | solution.py:38
  (2 shorter events, 0.0 us)
Async XLA Ops:
  6.5 17.8 %copy-start = (bf16[4096,32]{0,1:T(8,128)(2,1)S(1)}, bf16[4096,32]{0,1:T(8,128)(2,1)}, u32[]{:S(2)}) copy-start(bf16[4096,32]{0,1:T(8,128)(2,1)} %param.8) | copy-start | bytes 786436
  6.6 80.3 %all-reduce.11.cloned.1.call-start = ((), (), s32[]{:S(2)}) async-start(), calls=%async_computation.2 | async-start | bytes 6291456 | tf_op jit(solution)/shard_map/psum | solution.py:27
  6.6 9.3 %copy-start.3 = (f32[512,4096]{1,0:T(8,128)S(1)}, f32[512,4096]{1,0:T(8,128)}, u32[]{:S(2)}) copy-start(f32[512,4096]{1,0:T(8,128)} %param.6) | copy-start | bytes 25165828
  15.8 8.5 %copy-start.9 = (s32[1024]{0:T(1024)S(1)}, s32[1024]{0:T(1024)}, u32[]{:S(2)}) copy-start(s32[1024]{0:T(1024)} %param.11) | copy-start | bytes 12292
  15.8 8.5 %copy-start.7 = (f32[4096]{0:T(1024)S(1)}, f32[4096]{0:T(1024)}, u32[]{:S(2)}) copy-start(f32[4096]{0:T(1024)} %param.9) | copy-start | bytes 49156
  24.2 183.9 %all-reduce.9.cloned.1.call-start = ((), (), s32[]{:S(2)}) async-start(), calls=%async_computation.1 | async-start | bytes 6291456 | tf_op jit(solution)/shard_map/psum | solution.py:27
  97.1 12.0 %copy-start.4 = (f32[512,512]{1,0:T(8,128)S(1)}, f32[512,512]{1,0:T(8,128)}, u32[]{:S(2)}) copy-start(f32[512,512]{1,0:T(8,128)} %get-tuple-element.9) | copy-start | bytes 3145732
  97.1 12.0 %copy-start.8 = (f32[4096]{0:T(1024)S(1)}, f32[4096]{0:T(1024)}, u32[]{:S(2)}) copy-start(f32[4096]{0:T(1024)} %param.7) | copy-start | bytes 49156
  134.4 3.7 copy-start.2
  146.8 181.2 %all-reduce.7.cloned.1.call-start = ((), (), s32[]{:S(2)}) async-start(), calls=%async_computation | async-start | bytes 6291456 | tf_op jit(solution)/shard_map/psum | solution.py:27
  216.8 11.9 %copy-start.5 = (f32[512,512]{1,0:T(8,128)S(1)}, f32[512,512]{1,0:T(8,128)}, u32[]{:S(2)}) copy-start(f32[512,512]{1,0:T(8,128)} %get-tuple-element.7) | copy-start | bytes 3145732
  254.5 3.6 copy-start.1
  336.6 12.0 %copy-start.6 = (f32[512,512]{1,0:T(8,128)S(1)}, f32[512,512]{1,0:T(8,128)}, u32[]{:S(2)}) copy-start(f32[512,512]{1,0:T(8,128)} %get-tuple-element.5) | copy-start | bytes 3145732
Sparse Core Ops, SparseCore 0:
  24.4 62.4 all-reduce.10
  146.9 61.2 all-reduce.8
  266.7 61.1 all-reduce.6
where the time goes:
time: 391 us; the launch traced here: 383 us
  matrix products  170 us (43%)
  waiting for transfers between devices  87.7 us (22%)
  blocking collectives  83.6 us (21%)
  local copies, waits for them, and re-layouts  25.9 us (7%)
  between operations  13.5 us (3%)
    psum x3, waiting for transfers between devices, local_run(): lax.psum(lax.dot_general(part_bf, part_bf, DIMS_NT, preferred_element_typ...  87.6 us
    psum x3, blocking collectives, local_run(): lax.psum(jnp.dot(centred.astype(jnp.bfloat16), low_factor, preferred_elem...  83.6 us
    dot_general x3, matrix products, local_run(): jnp.dot(kern_bf, log_grad.astype(jnp.bfloat16), preferred_element_type=jn...  39.5 us
    dot_general x3, matrix products, local_run(): pulled = jnp.dot(kern_bf, part_bf, preferred_element_type=jnp.float32)  38.3 us
    dot_general x3, matrix products, local_run(): jnp.dot(residual.astype(jnp.bfloat16), data_mat, preferred_element_type=j...  35.9 us
    gather x3, local copies, waits for them, and re-layouts, local_run(): sq_norm = jnp.diagonal(gram_mat)  25.9 us
    dot_general x3, matrix products, local_run(): lax.dot_general(part_bf, data_mat, DIMS_NT, preferred_element_type=jnp.fl...  25.4 us
    dot_general x3, matrix products, local_run(): lax.dot_general(part_bf, part_bf, DIMS_NT, preferred_element_type=jnp.flo...  16.5 us
  transfers between devices with their start and end apart: 3, of which 3 were waited for; matrix products, arithmetic and copies ran while one was open for 4% of the time, Pallas kernels for 0%

commit v1 on v0

v1 whole, which is shorter than its diff:
```python
import functools
import math
import jax
import jax.numpy as jnp
from jax import lax
from jax.experimental import pallas as pl
from jax.experimental.pallas import tpu as pltpu
from jax.sharding import PartitionSpec as P

NUM_STEPS = 3
CORES = 2
F32, BF16 = jnp.float32, jnp.bfloat16
NN = (((1,), (0,)), ((), ()))
NT = (((1,), (1,)), ((), ()))
MESH = pl.DeviceIdType.MESH
KINDS = ("d2d", "s1a", "s1b", "ownb", "owna", "reda", "redb",
         "gr", "gl", "gp", "fa", "flp", "fb", "frp", "fop")


def dot(a, b, dims=NN):
    return lax.dot_general(a, b, dims, preferred_element_type=F32)


class Sum:
    def __init__(self, rows, half, width, part, pair, send, recv, full, sems, where, finish):
        self.rows, self.half, self.width = rows, half, width
        self.part, self.pair, self.send, self.recv, self.full = part, pair, send, recv, full
        self.ssem, self.rsem = sems
        self.core, self.chip, self.chips = where
        self.finish = finish

    def chip_at(self, hop):
        return lax.rem(self.chip + hop + self.chips, self.chips)

    def row(self, chip, core=None):
        core = self.core if core is None else core
        return pl.multiple_of((core * self.chips + chip) * self.rows, 8)

    def copy(self, kind, ch):
        rows, half = self.rows, self.half
        core, chip, chips = self.core, self.chip, self.chips
        right, left, opp = self.chip_at(1), self.chip_at(-1), self.chip_at(2)
        me = lambda c: {"feat": c * CORES + core}
        pair = {"feat": chip * CORES + (1 - core)}
        snd, rcv, full = self.send.at[ch], self.recv.at[ch], self.full.at[ch]
        block = lambda ref, lo, hi: ref.at[pl.ds(lo, hi - lo), :]

        def same(lo, size):
            ref = full.at[pl.ds(lo, size), :]
            return ref, ref
        if kind == "d2d":
            size = self.chips * rows
            src = self.part.at[ch].at[pl.ds(pl.multiple_of((1 - core) * size, 8), size), :]
            dst, dev = self.pair.at[ch], pair
        elif kind == "s1a":
            src, dst, dev = block(snd, 0, half), block(rcv, 0, half), me(right)
        elif kind == "s1b":
            src, dst, dev = block(snd, half, rows), block(rcv, half, rows), me(left)
        elif kind == "ownb":
            src, dst, dev = block(snd, rows + half, 2 * rows), block(rcv, rows + half, 2 * rows), me(right)
        elif kind == "owna":
            src, dst, dev = block(snd, 2 * rows, 2 * rows + half), block(rcv, 2 * rows, 2 * rows + half), me(left)
        elif kind == "reda":
            src, dst, dev = block(snd, rows, rows + half), block(rcv, rows, rows + half), me(right)
        elif kind == "redb":
            src, dst, dev = block(snd, 2 * rows + half, 3 * rows), block(rcv, 2 * rows + half, 3 * rows), me(left)
        elif kind == "gr":
            (src, dst), dev = same(self.row(chip), rows), me(right)
        elif kind == "gl":
            (src, dst), dev = same(self.row(chip), rows), me(left)
        elif kind == "gp":
            (src, dst), dev = same(self.row(chip), rows), pair
        elif kind == "fa":
            (src, dst), dev = same(self.row(left), half), me(right)
        elif kind == "flp":
            (src, dst), dev = same(self.row(left), rows), pair
        elif kind == "fb":
            (src, dst), dev = same(self.row(right) + half, rows - half), me(left)
        elif kind == "frp":
            (src, dst), dev = same(self.row(right), rows), pair
        elif kind == "fop":
            (src, dst), dev = same(self.row(opp), rows), pair
        k = KINDS.index(kind)
        return pltpu.make_async_remote_copy(
            src_ref=src, dst_ref=dst, send_sem=self.ssem.at[ch, k], recv_sem=self.rsem.at[ch, k],
            device_id=dev, device_id_type=MESH)

    def start(self, kind, ch):
        self.copy(kind, ch).start()

    def wait(self, kind, ch):
        self.copy(kind, ch).wait_recv()

    def mine(self, ch, chip, lo, hi):
        a = self.part[ch, pl.ds(self.row(chip) + lo, hi - lo), :]
        b = self.pair[ch, pl.ds(pl.multiple_of(chip * self.rows, 8) + lo, hi - lo), :]
        return a + b

    def put(self, ch, lo, value):
        self.send[ch, lo:lo + value.shape[0], :] = value.astype(self.send.dtype)

    def got(self, ch, lo, hi):
        return self.recv[ch, lo:hi, :].astype(F32)

    def stage(self, n, ch):
        rows, half = self.rows, self.half
        right, left, opp = self.chip_at(1), self.chip_at(-1), self.chip_at(2)
        if n == 0:
            self.start("d2d", ch)
        elif n == 1:
            self.wait("d2d", ch)
            self.put(ch, 0, self.mine(ch, opp, 0, rows))
            self.start("s1a", ch)
            self.start("s1b", ch)
            self.put(ch, rows + half, self.mine(ch, right, half, rows))
            self.start("ownb", ch)
            self.put(ch, 2 * rows, self.mine(ch, left, 0, half))
            self.start("owna", ch)
        elif n == 2:
            self.wait("s1a", ch)
            self.put(ch, rows, self.mine(ch, right, 0, half) + self.got(ch, 0, half))
            self.start("reda", ch)
            self.wait("s1b", ch)
            self.put(ch, 2 * rows + half, self.mine(ch, left, half, rows) + self.got(ch, half, rows))
            self.start("redb", ch)
        elif n == 3:
            for kind in ("ownb", "owna", "reda", "redb"):
                self.wait(kind, ch)
            total = self.mine(ch, self.chip, 0, rows) + self.got(ch, rows, 2 * rows) + self.got(ch, 2 * rows, 3 * rows)
            self.full[ch, pl.ds(self.row(self.chip), rows), :] = self.finish(ch, total)
            for kind in ("gr", "gl", "gp"):
                self.start(kind, ch)
        elif n == 4:
            self.wait("gr", ch)
            self.start("fa", ch)
            self.start("flp", ch)
            self.wait("gl", ch)
            self.start("fb", ch)
            self.start("frp", ch)
        elif n == 5:
            self.wait("fa", ch)
            self.wait("fb", ch)
            self.start("fop", ch)
        elif n == 6:
            for kind in ("gp", "flp", "frp", "fop"):
                self.wait(kind, ch)

    def drain(self, ch):
        for kind in KINDS:
            self.copy(kind, ch).wait_send()


def kernel(cfg, theta_hbm, lam_ref, mu_ref, ut_ref, a_hbm, y_ref, out_hbm,
           th, tb, av, sa, sb, kb, kv,
           zpart, zpair, zsend, zrecv, zfull, gpart, gpair, gsend, grecv, gfull,
           load_sem, store_sem, zss, zrs, gss, grs):
    chips, band, step, lik = cfg
    n_part, dim = th.shape
    m_rows = av.shape[0]
    nb = n_part // 2
    mc = m_rows // 2
    own = nb // (CORES * chips)
    tile = 1024
    rank = ut_ref.shape[0]
    me = lax.axis_index("feat")
    core, chip = lax.rem(me, CORES), me // CORES
    where = (core, chip, chips)

    def finish_z(ch, z):
        y = y_ref[:, (ch % 2) * mc:(ch % 2 + 1) * mc]
        return (y - 1.0 / (1.0 + jnp.exp(-z))).astype(BF16)

    zs = Sum(own, own // 2, mc, zpart, zpair, zsend, zrecv, zfull, (zss, zrs), where, finish_z)
    gs = Sum(own + 8, own // 2, nb, gpart, gpair, gsend, grecv, gfull, (gss, grs), where, lambda ch, g: g)

    def load_theta(i):
        return pltpu.make_async_copy(theta_hbm.at[pl.ds(i * nb, nb), :], th.at[pl.ds(i * nb, nb), :], load_sem.at[i])

    def load_a(j):
        return pltpu.make_async_copy(a_hbm.at[pl.ds(j * mc, mc), :], av.at[pl.ds(j * mc, mc), :], load_sem.at[2 + j])

    load_theta(0).start()
    load_a(0).start()
    load_theta(1).start()
    load_a(1).start()

    barrier = pltpu.get_barrier_semaphore()
    peers = (chip * CORES + (1 - core), zs.chip_at(1) * CORES + core, zs.chip_at(-1) * CORES + core)
    for peer in peers:
        pl.semaphore_signal(barrier, inc=1, device_id={"feat": peer}, device_id_type=MESH)

    gpart[...] = jnp.zeros_like(gpart)
    pl.semaphore_wait(barrier, len(peers))

    def tiles(body, width=tile):
        @pl.loop(0, dim // width)
        def _(t):
            body(pl.ds(pl.multiple_of(t * width, width), width))

    def rows(i):
        return slice(i * nb, (i + 1) * nb)

    def prep(i):
        load_theta(i).wait()

        def body(n):
            tb[rows(i), n] = th[rows(i), n].astype(BF16)
        tiles(body)

    def project(i):
        def body(t, acc):
            n = pl.ds(pl.multiple_of(t * tile, tile), tile)
            x = (th[rows(i), n] - mu_ref[:, n]).astype(BF16)
            return acc + dot(x, ut_ref[:, n], NT)
        q = lax.fori_loop(0, dim // tile, body, jnp.zeros((nb, rank), F32))
        ch = 2 * i
        fold = own // 8
        for o in range(CORES * chips):
            parts = [q[o * own + 8 * k:o * own + 8 * (k + 1)] for k in range(fold)]
            gpart[ch, o * (own + 8) + own:(o + 1) * (own + 8), 0:fold * rank] = jnp.concatenate(parts, axis=1)

    def gram(i):
        for j in range(i + 1):
            g = dot(tb[rows(i), :], tb[rows(j), :], NT)
            for o in range(CORES * chips):
                gpart[i + j, o * (own + 8):o * (own + 8) + own, :] = g[o * own:(o + 1) * own]

    def logit(i, j):
        zpart[2 * i + j] = dot(tb[rows(i), :], av[j * mc:(j + 1) * mc, :], NT)

    def low_rank(i):
        ch = 2 * i
        fold = own // 8
        parts = []
        for o in range(CORES * chips):
            p = gfull[ch, o * (own + 8) + own:(o + 1) * (own + 8), 0:128]
            parts += [p[:, rank * k:rank * (k + 1)] for k in range(fold)]
        q = jnp.concatenate(parts, axis=0).astype(BF16)

        def body(n):
            x = th[rows(i), n] - mu_ref[:, n]
            sa[rows(i), n] = -(x * lam_ref[:, n]) - dot(q, ut_ref[:, n])
        tiles(body)

    def lik_first(i):
        def body(n):
            sa[rows(i), n] = sa[rows(i), n] + lik * dot(zfull[2 * i], av[0:mc, n])
        tiles(body)

    def lik_last(i):
        def body(n):
            sb[rows(i), n] = (sa[rows(i), n] + lik * dot(zfull[2 * i + 1], av[mc:2 * mc, n])).astype(BF16)
        tiles(body)

    def kernel_mat():
        def gblock(ch):
            return jnp.concatenate(
                [gfull[ch, o * (own + 8):o * (own + 8) + own, :] for o in range(CORES * chips)], axis=0)

        def diag(g):
            eye = lax.broadcasted_iota(jnp.int32, g.shape, 0) == lax.broadcasted_iota(jnp.int32, g.shape, 1)
            d = jnp.where(eye, g, 0.0)
            return jnp.sum(d, axis=1, keepdims=True), jnp.sum(d, axis=0, keepdims=True)

        def rbf(c, r, g):
            return jnp.exp(-jnp.maximum(c + r - 2.0 * g, 0.0) / band)
        g00, g10, g11 = gblock(0), gblock(1), gblock(2)
        c0, r0 = diag(g00)
        c1, r1 = diag(g11)
        k00, k10, k11 = rbf(c0, r0, g00), rbf(c1, r0, g10), rbf(c1, r1, g11)
        k01 = k10.T
        kb[0:nb, 0:nb] = k00.astype(BF16)
        kb[0:nb, nb:] = k01.astype(BF16)
        kb[nb:, 0:nb] = k10.astype(BF16)
        kb[nb:, nb:] = k11.astype(BF16)
        kv[0:nb] = jnp.sum(k00, axis=1, keepdims=True) + jnp.sum(k01, axis=1, keepdims=True)
        kv[nb:] = jnp.sum(k10, axis=1, keepdims=True) + jnp.sum(k11, axis=1, keepdims=True)

    def pull(i):
        def body(n):
            t = th[rows(i), n]
            th[rows(i), n] = t + (step / n_part) * ((2.0 / band) * (kv[rows(i)] * t - dot(kb[rows(i), :], tb[:, n])))
        tiles(body)

    def drive(i, out=None):
        def body(n):
            t = th[rows(i), n] + (step / n_part) * dot(kb[rows(i), :], sb[:, n])
            th[rows(i), n] = t
            if out is None:
                tb[rows(i), n] = t.astype(BF16)
            else:
                out(n).start()
        tiles(body)

    def store(i):
        def out(n):
            return pltpu.make_async_copy(th.at[rows(i), n], out_hbm.at[rows(i), n], store_sem.at[i])
        return out

    @pl.loop(0, NUM_STEPS)
    def _(s):
        @pl.when(s == 0)
        def _():
            prep(0)
        project(0)
        gram(0)
        gs.stage(0, 0)

        @pl.when(s == 0)
        def _():
            load_a(0).wait()
        logit(0, 0)
        zs.stage(0, 0)
        gs.stage(1, 0)

        @pl.when(s == 0)
        def _():
            load_a(1).wait()
        logit(0, 1)
        zs.stage(0, 1)
        zs.stage(1, 0)
        gs.stage(2, 0)

        @pl.when(s == 0)
        def _():
            prep(1)

        @pl.when(s > 0)
        def _():
            drive(1)
        zs.stage(1, 1)
        zs.stage(2, 0)
        project(1)
        gs.stage(3, 0)
        gram(1)
        gs.stage(0, 1)
        gs.stage(0, 2)
        zs.stage(2, 1)
        zs.stage(3, 0)
        logit(1, 0)
        zs.stage(0, 2)
        gs.stage(1, 1)
        gs.stage(1, 2)
        gs.stage(4, 0)
        zs.stage(3, 1)
        logit(1, 1)
        zs.stage(0, 3)
        zs.stage(1, 2)
        gs.stage(2, 1)
        gs.stage(2, 2)
        zs.stage(4, 0)
        gs.stage(5, 0)
        gs.stage(6, 0)
        low_rank(0)
        zs.stage(1, 3)
        zs.stage(4, 1)
        gs.stage(3, 1)
        gs.stage(3, 2)
        zs.stage(5, 0)
        zs.stage(6, 0)
        lik_first(0)
        zs.stage(2, 2)
        zs.stage(2, 3)
        gs.stage(4, 1)
        gs.stage(4, 2)
        zs.stage(5, 1)
        zs.stage(6, 1)
        lik_last(0)
        zs.stage(3, 2)
        zs.stage(3, 3)
        gs.stage(5, 1)
        gs.stage(5, 2)
        gs.stage(6, 1)
        gs.stage(6, 2)
        low_rank(1)
        zs.stage(4, 2)
        kernel_mat()
        zs.stage(4, 3)
        zs.stage(5, 2)
        pull(0)
        zs.stage(5, 3)
        zs.stage(6, 2)
        pull(1)
        lik_first(1)
        zs.stage(6, 3)
        lik_last(1)
        for ch in range(4):
            zs.drain(ch)
        for ch in range(3):
            gs.drain(ch)

        @pl.when(s < NUM_STEPS - 1)
        def _():
            drive(0)

    drive(0, store(0))
    drive(1, store(1))
    for i in range(2):
        for t in range(dim // tile):
            store(i)(pl.ds(t * tile, tile)).wait()


def solution(mesh):
    feat_size = mesh.shape["feat"]
    chips = feat_size // CORES

    def local_run(particles, prec_diag, low_factor, prior_mean, data_mat, labels):
        n_part, dim = particles.shape
        m_rows = data_mat.shape[0]
        rank = low_factor.shape[1]
        dim_full = dim * feat_size
        cfg = (chips, 2.0 * dim_full, dim_full / 4.0, 2.0 / math.sqrt(m_rows * dim_full))
        nb, mc = n_part // 2, m_rows // 2
        own = nb // feat_size
        vm, any_ = pl.BlockSpec(memory_space=pltpu.VMEM), pl.BlockSpec(memory_space=pl.ANY)
        dma = pltpu.SemaphoreType.DMA
        scratch = [
            pltpu.VMEM((n_part, dim), F32), pltpu.VMEM((n_part, dim), BF16), pltpu.VMEM((m_rows, dim), BF16),
            pltpu.VMEM((n_part, dim), F32), pltpu.VMEM((n_part, dim), BF16),
            pltpu.VMEM((n_part, n_part), BF16), pltpu.VMEM((n_part, 1), F32),
        ]
        for count, rows, width, wire in ((4, own, mc, BF16), (3, own + 8, nb, F32)):
            scratch += [
                pltpu.VMEM((count, feat_size * rows, width), F32), pltpu.VMEM((count, chips * rows, width), F32),
                pltpu.VMEM((count, 3 * rows, width), wire), pltpu.VMEM((count, 3 * rows, width), wire),
                pltpu.VMEM((count, feat_size * rows, width), wire),
            ]
        scratch += [dma((4,)), dma((2,))] + [dma((4, len(KINDS)))] * 2 + [dma((3, len(KINDS)))] * 2
        return pl.pallas_call(
            functools.partial(kernel, cfg),
            out_shape=jax.ShapeDtypeStruct((n_part, dim), F32),
            in_specs=[any_, vm, vm, vm, any_, vm],
            out_specs=any_,
            scratch_shapes=scratch,
            compiler_params=pltpu.CompilerParams(
                collective_id=0, has_side_effects=True, vmem_limit_bytes=60 * 2**20),
            cost_estimate=pl.CostEstimate(flops=60 * 10**9, bytes_accessed=32 * 2**20, transcendentals=0),
        )(particles, prec_diag[None, :], prior_mean[None, :], low_factor.T, data_mat, labels.astype(F32)[None, :])

    return jax.shard_map(
        local_run,
        mesh=mesh,
        in_specs=(P("ens", "feat"), P(("ens", "feat")), P(("ens", "feat"), None),
                  P(("ens", "feat")), P("ens", "feat"), P("ens")),
        out_specs=P("ens", "feat"),
        check_vma=False,
    )
```

time: 391 us -> 151 us (0.39); the launches traced: 383 us -> 151 us
  matrix products: 170 us -> 0 us
  Pallas kernels: 0 us -> 142 us
  waiting for transfers between devices: 87.7 us -> 0 us
  blocking collectives: 83.6 us -> 0 us
  local copies, waits for them, and re-layouts: 25.9 us -> 7.77 us
  between operations: 13.5 us -> 0.01 us
    dot_general x18 -> x0, matrix products: 170 us -> none  [the longest x3 39.5 us: local_run(): jnp.dot(kern_bf, log_grad.astype(jnp.bfloat16), preferred_element_type=jn...]
    pallas_call x0 -> x1, Pallas kernels: none -> 142 us  [local_run(): pl.pallas_call(functools.partial(kernel, cfg), out_shape=jax.ShapeDtypeSt...]
    psum x3 -> x0, waiting for transfers between devices: 87.6 us -> none  [local_run(): lax.psum(lax.dot_general(part_bf, part_bf, DIMS_NT, preferred_element_typ...]
    psum x3 -> x0, blocking collectives: 83.6 us -> none  [local_run(): lax.psum(jnp.dot(centred.astype(jnp.bfloat16), low_factor, preferred_elem...]
    gather x3 -> x0, local copies, waits for them, and re-layouts: 25.9 us -> none  [local_run(): sq_norm = jnp.diagonal(gram_mat)]
    unnamed x20 -> x1, local copies, waits for them, and re-layouts: 0.04 us -> 7.77 us
  transfers between devices with their start and end apart: 3 -> 0, of which waited for: 3 -> 0; matrix products, arithmetic and copies ran while one was open for 4% -> 0% of each run, Pallas kernels for 0% -> 0%
where the time goes in v1:
time: 151 us
  Pallas kernels  142 us (94%)
  local copies, waits for them, and re-layouts  7.77 us (5%)
    pallas_call x1, Pallas kernels, local_run(): pl.pallas_call(functools.partial(kernel, cfg), out_shape=jax.ShapeDtypeSt...  142 us
    unnamed x1, local copies, waits for them, and re-layouts  7.77 us

profile of v1, /device:TPU:113, one launch (start us, length us, event | category | flops | bytes accessed | tf_op | source)
XLA Modules:
  0.0 151.0 jit_solution(6072400134564656919)
XLA Ops:
  0.0 1.3 convert_element_type.3
  1.3 142.0 %shard_map.64 = f32[512,4096]{1,0:T(8,128)} custom-call(f32[512,4096]{1,0:T(8,128)} %theta_hbm.1, f32[1,4096]{1,0:T(1,128)} %bitcast.6, f32[1,4096]{1,0:T(1,128)} %bitcast.7, bf16[32,4096]{1,0:T(8,128)(2,1)} %bitcast.5, bf16[1024,4096]{1,0:T(8,128)(2,1)} %a_hbm.1, f32[1,1024]{1,0:T(1,128)} %bitcast.4), custom_call_target="tpu_custom_call" | custom-call | flops 60000002048 | bytes 33554432 | tf_op jit(solution)/shard_map/pallas_call | solution.py:429
  143.3 7.8 %copy.8 = f32[512,4096]{1,0:T(8,128)} copy(f32[512,4096]{1,0:T(8,128)} %shard_map.64) | data formatting | bytes 16777216

commit v2 on v0

v2 whole, which is shorter than its diff:
```python
import functools
import math
import jax
import jax.numpy as jnp
from jax import lax
from jax.experimental import pallas as pl
from jax.experimental.pallas import tpu as pltpu
from jax.sharding import PartitionSpec as P

NUM_STEPS = 3
CORES = 2
LANES = 128
F32, BF16 = jnp.float32, jnp.bfloat16
NN = (((1,), (0,)), ((), ()))
NT = (((1,), (1,)), ((), ()))
MESH = pl.DeviceIdType.MESH
KINDS = ("d2d", "s1a", "s1b", "ownb", "owna", "reda", "redb",
         "gr", "gl", "gp", "fa", "flp", "fb", "frp", "fop")
DIRECT_KINDS = ("d2d", "ir", "il", "io", "gr", "gl", "go", "gp", "flp", "frp", "fop")
CHUNKS = ("g0", "z0", "z3", "g1", "z1", "z2")
DIRECT = ('g0', 'g1', 'z0', 'z1', 'z2', 'z3')
SCHEDULE = (
    "z0q", "z3:0", "z0p", "z0:0", "z3:1", "gram0", "g0:0", "drive1a", "z0:1", "drive1b", "g0:1", "z1",
    "z1:0", "proj1", "z3:3", "gram1", "z0:3", "proj0", "z1:1", "g1:0", "z2", "g1:1", "z0:4", "z2:0",
    "z3:4", "z3:5", "z1:3", "z0:5", "z3:6", "z0:6", "z2:1", "g1:3", "z1:4", "z1:5", "z2:3", "z1:6",
    "l0a", "g0:3", "l0b", "g1:4", "g1:5", "lf1a", "lf1b", "z2:4", "z2:5", "g1:6", "lr0", "lr1",
    "g0:4", "z2:6", "g0:5", "ll1a", "ll1b", "g0:6", "kmat", "drive0a", "drive0b",
)


def dot(a, b, dims=NN):
    return lax.dot_general(a, b, dims, preferred_element_type=F32)


class Chunk:
    def __init__(self, name, bufs, where, finish):
        self.part, self.pair, self.send, self.recv, self.full, self.ssem, self.rsem = bufs
        self.core, self.chip, self.chips = where
        self.rows = self.full.shape[0] // (CORES * self.chips)
        self.half = self.rows // 32 * 16
        self.direct = name in DIRECT
        self.kinds = DIRECT_KINDS if self.direct else KINDS
        self.finish = finish

    def chip_at(self, hop):
        return lax.rem(self.chip + hop + self.chips, self.chips)

    def row(self, chip):
        return pl.multiple_of((self.core * self.chips + chip) * self.rows, 8)

    def copy(self, kind):
        rows, half = self.rows, self.half
        core, chip = self.core, self.chip
        right, left, opp = self.chip_at(1), self.chip_at(-1), self.chip_at(2)
        at = lambda c: {"feat": c * CORES + core}
        pair = {"feat": chip * CORES + (1 - core)}
        snd, rcv, full = self.send, self.recv, self.full

        def same(lo, size):
            ref = full.at[pl.ds(lo, size), :]
            return ref, ref

        def slot(lo, hi):
            return snd.at[pl.ds(lo, hi - lo), :], rcv.at[pl.ds(lo, hi - lo), :]

        if kind == "d2d":
            size = self.chips * rows
            src, dst = self.part.at[pl.ds(pl.multiple_of((1 - core) * size, 8), size), :], self.pair
            dev = pair
        else:
            (src, dst), dev = {
                "s1a": lambda: (slot(0, half), at(right)),
                "s1b": lambda: (slot(half, rows), at(left)),
                "ownb": lambda: (slot(rows + half, 2 * rows), at(right)),
                "owna": lambda: (slot(2 * rows, 2 * rows + half), at(left)),
                "reda": lambda: (slot(rows, rows + half), at(right)),
                "redb": lambda: (slot(2 * rows + half, 3 * rows), at(left)),
                "io": lambda: (slot(0, rows), at(opp)),
                "ir": lambda: (slot(rows, 2 * rows), at(right)),
                "il": lambda: (slot(2 * rows, 3 * rows), at(left)),
                "gr": lambda: (same(self.row(chip), rows), at(right)),
                "gl": lambda: (same(self.row(chip), rows), at(left)),
                "go": lambda: (same(self.row(chip), rows), at(opp)),
                "gp": lambda: (same(self.row(chip), rows), pair),
                "fa": lambda: (same(self.row(left), half), at(right)),
                "flp": lambda: (same(self.row(left), rows), pair),
                "fb": lambda: (same(self.row(right) + half, rows - half), at(left)),
                "frp": lambda: (same(self.row(right), rows), pair),
                "fop": lambda: (same(self.row(opp), rows), pair),
            }[kind]()
        k = self.kinds.index(kind)
        return pltpu.make_async_remote_copy(
            src_ref=src, dst_ref=dst, send_sem=self.ssem.at[k], recv_sem=self.rsem.at[k],
            device_id=dev, device_id_type=MESH)

    def start(self, *kinds):
        for kind in kinds:
            self.copy(kind).start()

    def wait(self, *kinds):
        for kind in kinds:
            self.copy(kind).wait_recv()

    def mine(self, chip, lo, hi):
        a = self.part[pl.ds(self.row(chip) + lo, hi - lo), :]
        b = self.pair[pl.ds(pl.multiple_of(chip * self.rows, 8) + lo, hi - lo), :]
        return a + b

    def put(self, lo, value):
        self.send[lo:lo + value.shape[0], :] = value.astype(self.send.dtype)

    def got(self, lo, hi):
        return self.recv[lo:hi, :].astype(F32)

    def stage(self, n):
        rows, half = self.rows, self.half
        right, left, opp = self.chip_at(1), self.chip_at(-1), self.chip_at(2)
        if n == 0:
            self.start("d2d")
        elif n == 1:
            self.wait("d2d")
            self.put(0, self.mine(opp, 0, rows))
            if self.direct:
                self.start("io")
                self.put(rows, self.mine(right, 0, rows))
                self.start("ir")
                self.put(2 * rows, self.mine(left, 0, rows))
                self.start("il")
            else:
                self.start("s1a", "s1b")
                self.put(rows + half, self.mine(right, half, rows))
                self.start("ownb")
                self.put(2 * rows, self.mine(left, 0, half))
                self.start("owna")
        elif n == 2:
            self.wait("s1a")
            self.put(rows, self.mine(right, 0, half) + self.got(0, half))
            self.start("reda")
            self.wait("s1b")
            self.put(2 * rows + half, self.mine(left, half, rows) + self.got(half, rows))
            self.start("redb")
        elif n == 3:
            total = self.mine(self.chip, 0, rows)
            if self.direct:
                self.wait("ir", "il", "io")
                total = total + self.got(rows, 2 * rows) + self.got(2 * rows, 3 * rows) + self.got(0, rows)
            else:
                self.wait("ownb", "owna", "reda", "redb")
                total = total + self.got(rows, 2 * rows) + self.got(2 * rows, 3 * rows)
            self.full[pl.ds(self.row(self.chip), rows), :] = self.finish(total)
            if self.direct:
                self.start("go")
            self.start("gr", "gl", "gp")
        elif n == 4:
            self.wait("gr")
            if not self.direct:
                self.start("fa")
            self.start("flp")
            self.wait("gl")
            if not self.direct:
                self.start("fb")
            self.start("frp")
        elif n == 5:
            if self.direct:
                self.wait("go")
            else:
                self.wait("fa", "fb")
            self.start("fop")
        elif n == 6:
            self.wait("gp", "flp", "frp", "fop")

    def drain(self):
        for kind in self.kinds:
            self.copy(kind).wait_send()


def kernel(cfg, theta_hbm, lam_ref, mu_ref, ut_ref, a_hbm, y_ref, out_hbm, th, tb, av, sa, sb, kb, kv,
           load_sem, store_sem, *chunk_bufs):
    chips, band, step, lik = cfg
    n_part, dim = th.shape
    m_rows = av.shape[0]
    nb, mc = n_part // 2, m_rows // 2
    owners = CORES * chips
    own = nb // owners
    wide, sub = dim // 2, 512
    rank = ut_ref.shape[0]
    pack = LANES // rank
    pull = 2.0 / band
    gain = step / n_part
    me = lax.axis_index("feat")
    where = (lax.rem(me, CORES), me // CORES, chips)

    def finish(name):
        if name[0] == "g":
            return lambda g: g
        lo = 0 if name in ("z0", "z1") else mc

        def residual(z):
            return (y_ref[:, lo:lo + mc].astype(F32) - 1.0 / (1.0 + jnp.exp(-z))).astype(BF16)
        return residual

    ch = {}
    for k, name in enumerate(CHUNKS):
        ch[name] = Chunk(name, chunk_bufs[7 * k:7 * k + 7], where, finish(name))

    def rows(i):
        return slice(i * nb, (i + 1) * nb)

    def load_theta(i):
        return pltpu.make_async_copy(theta_hbm.at[pl.ds(i * nb, nb), :], th.at[pl.ds(i * nb, nb), :], load_sem.at[i])

    def load_a(j):
        return pltpu.make_async_copy(a_hbm.at[pl.ds(j * mc, mc), :], av.at[pl.ds(j * mc, mc), :], load_sem.at[2 + j])

    load_theta(0).start()
    load_a(0).start()
    load_a(1).start()
    load_theta(1).start()

    any_chunk = ch[CHUNKS[0]]
    barrier = pltpu.get_barrier_semaphore()
    peers = [where[1] * CORES + (1 - where[0])]
    peers += [any_chunk.chip_at(hop) * CORES + where[0] for hop in (1, -1, 2)]
    for peer in peers:
        pl.semaphore_signal(barrier, inc=1, device_id={"feat": peer}, device_id_type=MESH)
    pl.semaphore_wait(barrier, len(peers))

    def columns(lo, hi):
        return [slice(n, n + sub) for n in range(lo, hi, sub)]

    def prep(i):
        load_theta(i).wait()

        @pl.loop(0, dim // wide)
        def _(t):
            n = pl.ds(pl.multiple_of(t * wide, wide), wide)
            tb[rows(i), n] = th[rows(i), n].astype(BF16)

    def project(i):
        q = jnp.zeros((nb, rank), F32)
        for n in columns(0, dim):
            q = q + dot((th[rows(i), n] - mu_ref[:, n]).astype(BF16), ut_ref[:, n], NT)
        piece = 2 * own + 8
        for o in range(owners):
            parts = [q[o * own + 8 * k:o * own + 8 * (k + 1)] for k in range(pack)]
            ch["g1"].part[o * piece + 2 * own:(o + 1) * piece, i * LANES:(i + 1) * LANES] = \
                jnp.concatenate(parts, axis=1)

    def gram(i):
        g = dot(tb[rows(i), :], tb[0:(i + 1) * nb, :], NT)
        part = ch[f"g{i}"].part
        piece = part.shape[0] // owners
        for j in range(i + 1):
            for o in range(owners):
                part[o * piece + j * own:o * piece + (j + 1) * own, :] = g[o * own:(o + 1) * own, j * nb:(j + 1) * nb]

    def logit(name, i, j):
        ch[name].part[...] = dot(tb[rows(i), :], av[j * mc:(j + 1) * mc, :], NT)

    def base(i, n, q):
        t = th[rows(i), n]
        return -((t - mu_ref[:, n]) * lam_ref[:, n]) - dot(q, ut_ref[:, n]) - pull * tb[rows(i), n].astype(F32)

    def gathered_q(i):
        piece = 2 * own + 8
        parts = []
        for o in range(owners):
            p = ch["g1"].full[o * piece + 2 * own:(o + 1) * piece, i * LANES:(i + 1) * LANES]
            parts += [p[:, rank * k:rank * (k + 1)] for k in range(pack)]
        return jnp.concatenate(parts, axis=0).astype(BF16)

    def both_lik(lo, hi):
        for n in columns(lo, hi):
            sa[rows(0), n] = lik * (dot(ch["z0"].full[...], av[0:mc, n]) + dot(ch["z3"].full[...], av[mc:2 * mc, n]))

    def first_lik(lo, hi):
        for n in columns(lo, hi):
            sa[rows(1), n] = lik * dot(ch["z1"].full[...], av[0:mc, n])

    def last_lik(lo, hi):
        for n in columns(lo, hi):
            sb[rows(1), n] = (sa[rows(1), n] + lik * dot(ch["z2"].full[...], av[mc:2 * mc, n])).astype(BF16)

    def low_rank(i):
        q = gathered_q(i)
        for n in columns(0, dim):
            s = sa[rows(i), n] + base(i, n, q)
            if i == 0:
                sb[rows(i), n] = s.astype(BF16)
            else:
                sa[rows(i), n] = s

    def kernel_mat():
        def block(name, j):
            full = ch[name].full
            piece = full.shape[0] // owners
            return jnp.concatenate(
                [full[o * piece + j * own:o * piece + (j + 1) * own, :] for o in range(owners)], axis=0)

        def diag(g):
            eye = lax.broadcasted_iota(jnp.int32, g.shape, 0) == lax.broadcasted_iota(jnp.int32, g.shape, 1)
            d = jnp.where(eye, g, 0.0)
            return jnp.sum(d, axis=1, keepdims=True), jnp.sum(d, axis=0, keepdims=True)

        def rbf(c, r, g):
            return jnp.exp(-jnp.maximum(c + r - 2.0 * g, 0.0) / band)

        g00, g10, g11 = block("g0", 0), block("g1", 0), block("g1", 1)
        (c0, r0), (c1, r1) = diag(g00), diag(g11)
        k00, k10, k11 = rbf(c0, r0, g00), rbf(c1, r0, g10), rbf(c1, r1, g11)
        k01 = k10.T
        for i, j, k in ((0, 0, k00), (0, 1, k01), (1, 0, k10), (1, 1, k11)):
            kb[rows(i), rows(j)] = k.astype(BF16)
        for i, pair in ((0, (k00, k01)), (1, (k10, k11))):
            total = jnp.sum(pair[0], axis=1, keepdims=True) + jnp.sum(pair[1], axis=1, keepdims=True)
            kv[rows(i), :] = jnp.broadcast_to(gain * pull * total, (nb, LANES))

    def drive(i, lo, hi, out=False):
        for n in columns(lo, hi):
            t = th[rows(i), n]
            scale = jnp.concatenate([kv[rows(i), :]] * (sub // LANES), axis=1)
            t = t + (scale * t + gain * dot(kb[rows(i), :], sb[:, n]))
            th[rows(i), n] = t
            if not out:
                tb[rows(i), n] = t.astype(BF16)

    def store(i, lo, hi):
        n = pl.ds(lo, hi - lo)
        return pltpu.make_async_copy(th.at[rows(i), n], out_hbm.at[rows(i), n], store_sem.at[2 * i + lo // (hi - lo)])

    halves = {"a": (0, wide), "b": (wide, dim)}
    pieces = {
        "proj0": lambda: project(0), "proj1": lambda: project(1), "gram0": lambda: gram(0), "gram1": lambda: gram(1),
        "z0p": lambda: logit("z0", 0, 0), "z0q": lambda: logit("z3", 0, 1),
        "z1": lambda: logit("z1", 1, 0), "z2": lambda: logit("z2", 1, 1),
        "lr0": lambda: low_rank(0), "lr1": lambda: low_rank(1), "kmat": kernel_mat,
    }
    for h, (lo, hi) in halves.items():
        pieces["l0" + h] = functools.partial(both_lik, lo, hi)
        pieces["lf1" + h] = functools.partial(first_lik, lo, hi)
        pieces["ll1" + h] = functools.partial(last_lik, lo, hi)
        pieces["drive0" + h] = functools.partial(drive, 0, lo, hi)
        pieces["drive1" + h] = functools.partial(drive, 1, lo, hi)

    @pl.loop(0, NUM_STEPS)
    def _(s):
        @pl.when(s == 0)
        def _():
            prep(0)

        loaded = set()
        for item in SCHEDULE:
            if ":" in item:
                name, n = item.split(":")
                ch[name].stage(int(n))
                continue
            if item in ("z0p", "z0q"):
                @pl.when(s == 0)
                def _():
                    load_a("pq".index(item[-1])).wait()
            if item == "drive1a":
                @pl.when(s == 0)
                def _():
                    prep(1)
            if item[:6] == "drive1":
                pl.when(s > 0)(pieces[item])
            elif item[:6] == "drive0":
                pl.when(s < NUM_STEPS - 1)(pieces[item])
            else:
                pieces[item]()
        for name in CHUNKS:
            ch[name].drain()

    for i in range(2):
        for lo, hi in halves.values():
            drive(i, lo, hi, out=True)
            store(i, lo, hi).start()
    for i in range(2):
        for lo, hi in halves.values():
            store(i, lo, hi).wait()


def solution(mesh):
    feat_size = mesh.shape["feat"]
    chips = feat_size // CORES

    def local_run(particles, prec_diag, low_factor, prior_mean, data_mat, labels):
        n_part, dim = particles.shape
        m_rows = data_mat.shape[0]
        dim_full = dim * feat_size
        cfg = (chips, 2.0 * dim_full, dim_full / 4.0, 2.0 / math.sqrt(m_rows * dim_full))
        nb, mc = n_part // 2, m_rows // 2
        own = nb // feat_size
        vm, any_ = pl.BlockSpec(memory_space=pltpu.VMEM), pl.BlockSpec(memory_space=pl.ANY)
        dma = pltpu.SemaphoreType.DMA
        scratch = [
            pltpu.VMEM((n_part, dim), F32), pltpu.VMEM((n_part, dim), BF16), pltpu.VMEM((m_rows, dim), BF16),
            pltpu.VMEM((n_part, dim), F32), pltpu.VMEM((n_part, dim), BF16),
            pltpu.VMEM((n_part, n_part), BF16), pltpu.VMEM((n_part, LANES), F32), dma((4,)), dma((4,)),
        ]
        for name in CHUNKS:
            wire, width, rows = (F32, nb, own) if name[0] == "g" else (BF16, mc, own)
            if name == "g1":
                rows = 2 * own + 8
            count = len(DIRECT_KINDS if name in DIRECT else KINDS)
            scratch += [
                pltpu.VMEM((feat_size * rows, width), F32), pltpu.VMEM((chips * rows, width), F32),
                pltpu.VMEM((3 * rows, width), wire), pltpu.VMEM((3 * rows, width), wire),
                pltpu.VMEM((feat_size * rows, width), wire), dma((count,)), dma((count,)),
            ]
        return pl.pallas_call(
            functools.partial(kernel, cfg),
            out_shape=jax.ShapeDtypeStruct((n_part, dim), F32),
            in_specs=[any_, vm, vm, vm, any_, vm],
            out_specs=any_,
            scratch_shapes=scratch,
            compiler_params=pltpu.CompilerParams(
                collective_id=0, has_side_effects=True, vmem_limit_bytes=60 * 2**20),
            cost_estimate=pl.CostEstimate(flops=60 * 10**9, bytes_accessed=32 * 2**20, transcendentals=0),
        )(particles, prec_diag[None, :], prior_mean[None, :], low_factor.T, data_mat, labels[None, :])

    return jax.shard_map(
        local_run,
        mesh=mesh,
        in_specs=(P("ens", "feat"), P(("ens", "feat")), P(("ens", "feat"), None),
                  P(("ens", "feat")), P("ens", "feat"), P("ens")),
        out_specs=P("ens", "feat"),
        check_vma=False,
    )
```

time: 391 us -> 119 us (0.30); the launches traced: 383 us -> 118 us
  matrix products: 170 us -> 0 us
  Pallas kernels: 0 us -> 111 us
  waiting for transfers between devices: 87.7 us -> 0 us
  blocking collectives: 83.6 us -> 0 us
  local copies, waits for them, and re-layouts: 25.9 us -> 7.77 us
  between operations: 13.5 us -> 0.01 us
    dot_general x18 -> x0, matrix products: 170 us -> none  [the longest x3 39.5 us: local_run(): jnp.dot(kern_bf, log_grad.astype(jnp.bfloat16), preferred_element_type=jn...]
    pallas_call x0 -> x1, Pallas kernels: none -> 111 us  [local_run(): pl.pallas_call(functools.partial(kernel, cfg), out_shape=jax.ShapeDtypeSt...]
    psum x3 -> x0, waiting for transfers between devices: 87.6 us -> none  [local_run(): lax.psum(lax.dot_general(part_bf, part_bf, DIMS_NT, preferred_element_typ...]
    psum x3 -> x0, blocking collectives: 83.6 us -> none  [local_run(): lax.psum(jnp.dot(centred.astype(jnp.bfloat16), low_factor, preferred_elem...]
    gather x3 -> x0, local copies, waits for them, and re-layouts: 25.9 us -> none  [local_run(): sq_norm = jnp.diagonal(gram_mat)]
    unnamed x20 -> x1, local copies, waits for them, and re-layouts: 0.04 us -> 7.77 us
  transfers between devices with their start and end apart: 3 -> 0, of which waited for: 3 -> 0; matrix products, arithmetic and copies ran while one was open for 4% -> 0% of each run, Pallas kernels for 0% -> 0%
where the time goes in v2:
time: 119 us; the launch traced here: 118 us
  Pallas kernels  111 us (93%)
  local copies, waits for them, and re-layouts  7.77 us (7%)
    pallas_call x1, Pallas kernels, local_run(): pl.pallas_call(functools.partial(kernel, cfg), out_shape=jax.ShapeDtypeSt...  111 us
    unnamed x1, local copies, waits for them, and re-layouts  7.77 us

profile of v2, /device:TPU:113, one launch (start us, length us, event | category | flops | bytes accessed | tf_op | source)
XLA Modules:
  0.0 118.5 jit_solution(7656010868793633921)
XLA Ops:
  0.0 110.7 %shard_map.64 = f32[512,4096]{1,0:T(8,128)} custom-call(f32[512,4096]{1,0:T(8,128)} %theta_hbm.1, f32[1,4096]{1,0:T(1,128)} %bitcast.5, f32[1,4096]{1,0:T(1,128)} %bitcast.6, bf16[32,4096]{1,0:T(8,128)(2,1)} %bitcast.4, bf16[1024,4096]{1,0:T(8,128)(2,1)} %a_hbm.1, s32[1,1024]{1,0:T(1,128)} %bitcast.7), custom_call_target="tpu_custom_call" | custom-call | flops 60000002048 | bytes 33554432 | tf_op jit(solution)/shard_map/pallas_call | solution.py:411
  110.7 7.8 %copy.8 = f32[512,4096]{1,0:T(8,128)} copy(f32[512,4096]{1,0:T(8,128)} %shard_map.64) | data formatting | bytes 16777216

commit v3 on v2

--- a/solution.py
+++ b/solution.py
@@ -13,18 +13,18 @@
 F32, BF16 = jnp.float32, jnp.bfloat16
 NN = (((1,), (0,)), ((), ()))
 NT = (((1,), (1,)), ((), ()))
-MESH = pl.DeviceIdType.MESH
+LOGICAL = pl.DeviceIdType.LOGICAL
 KINDS = ("d2d", "s1a", "s1b", "ownb", "owna", "reda", "redb",
          "gr", "gl", "gp", "fa", "flp", "fb", "frp", "fop")
 DIRECT_KINDS = ("d2d", "ir", "il", "io", "gr", "gl", "go", "gp", "flp", "frp", "fop")
 CHUNKS = ("g0", "z0", "z3", "g1", "z1", "z2")
 DIRECT = ('g0', 'g1', 'z0', 'z1', 'z2', 'z3')
 SCHEDULE = (
-    "z0q", "z3:0", "z0p", "z0:0", "z3:1", "gram0", "g0:0", "drive1a", "z0:1", "drive1b", "g0:1", "z1",
-    "z1:0", "proj1", "z3:3", "gram1", "z0:3", "proj0", "z1:1", "g1:0", "z2", "g1:1", "z0:4", "z2:0",
-    "z3:4", "z3:5", "z1:3", "z0:5", "z3:6", "z0:6", "z2:1", "g1:3", "z1:4", "z1:5", "z2:3", "z1:6",
-    "l0a", "g0:3", "l0b", "g1:4", "g1:5", "lf1a", "lf1b", "z2:4", "z2:5", "g1:6", "lr0", "lr1",
-    "g0:4", "z2:6", "g0:5", "ll1a", "ll1b", "g0:6", "kmat", "drive0a", "drive0b",
+    "z0q", "z3:0", "z0p", "z0:0", "z3:1", "gram0", "z0:1", "g0:0", "drive1a", "drive1b", "g0:1", "z1",
+    "z3:3", "z1:0", "gram1", "z0:3", "proj", "g1:0", "z1:1", "g1:1", "z3:4", "z3:5", "z2", "z0:4",
+    "z1:3", "z0:5", "z2:0", "z2:1", "z3:6", "g1:3", "z0:6", "z1:4", "l0a", "z2:3", "g0:3", "z1:5",
+    "l0b", "z1:6", "lf1a", "lf1b", "g1:4", "g1:5", "z2:4", "z2:5", "g1:6", "lr1", "z2:6", "ll1a",
+    "g0:4", "g0:5", "ll1b", "lr0", "g0:6", "kmat", "drive0a", "drive0b",
 )
 
 
@@ -35,25 +35,21 @@
 class Chunk:
     def __init__(self, name, bufs, where, finish):
         self.part, self.pair, self.send, self.recv, self.full, self.ssem, self.rsem = bufs
-        self.core, self.chip, self.chips = where
+        self.core, self.chip, self.chips, self.chip_of, self.ids = where
         self.rows = self.full.shape[0] // (CORES * self.chips)
         self.half = self.rows // 32 * 16
         self.direct = name in DIRECT
         self.kinds = DIRECT_KINDS if self.direct else KINDS
         self.finish = finish
 
-    def chip_at(self, hop):
-        return lax.rem(self.chip + hop + self.chips, self.chips)
-
-    def row(self, chip):
-        return pl.multiple_of((self.core * self.chips + chip) * self.rows, 8)
+    def row(self, hop):
+        return pl.multiple_of((self.core * self.chips + self.chip_of[hop]) * self.rows, 8)
 
     def copy(self, kind):
         rows, half = self.rows, self.half
-        core, chip = self.core, self.chip
-        right, left, opp = self.chip_at(1), self.chip_at(-1), self.chip_at(2)
-        at = lambda c: {"feat": c * CORES + core}
-        pair = {"feat": chip * CORES + (1 - core)}
+        core, pair = self.core, self.ids["pair"]
+        chip, right, left, opp = 0, 1, -1, 2
+        at = lambda hop: self.ids[hop]
         snd, rcv, full = self.send, self.recv, self.full
 
         def same(lo, size):
@@ -91,7 +87,7 @@
         k = self.kinds.index(kind)
         return pltpu.make_async_remote_copy(
             src_ref=src, dst_ref=dst, send_sem=self.ssem.at[k], recv_sem=self.rsem.at[k],
-            device_id=dev, device_id_type=MESH)
+            device_id=dev, device_id_type=LOGICAL)
 
     def start(self, *kinds):
         for kind in kinds:
@@ -101,9 +97,9 @@
         for kind in kinds:
             self.copy(kind).wait_recv()
 
-    def mine(self, chip, lo, hi):
-        a = self.part[pl.ds(self.row(chip) + lo, hi - lo), :]
-        b = self.pair[pl.ds(pl.multiple_of(chip * self.rows, 8) + lo, hi - lo), :]
+    def mine(self, hop, lo, hi):
+        a = self.part[pl.ds(self.row(hop) + lo, hi - lo), :]
+        b = self.pair[pl.ds(pl.multiple_of(self.chip_of[hop] * self.rows, 8) + lo, hi - lo), :]
         return a + b
 
     def put(self, lo, value):
@@ -114,7 +110,7 @@
 
     def stage(self, n):
         rows, half = self.rows, self.half
-        right, left, opp = self.chip_at(1), self.chip_at(-1), self.chip_at(2)
+        right, left, opp = 1, -1, 2
         if n == 0:
             self.start("d2d")
         elif n == 1:
@@ -140,14 +136,14 @@
             self.put(2 * rows + half, self.mine(left, half, rows) + self.got(half, rows))
             self.start("redb")
         elif n == 3:
-            total = self.mine(self.chip, 0, rows)
+            total = self.mine(0, 0, rows)
             if self.direct:
                 self.wait("ir", "il", "io")
                 total = total + self.got(rows, 2 * rows) + self.got(2 * rows, 3 * rows) + self.got(0, rows)
             else:
                 self.wait("ownb", "owna", "reda", "redb")
                 total = total + self.got(rows, 2 * rows) + self.got(2 * rows, 3 * rows)
-            self.full[pl.ds(self.row(self.chip), rows), :] = self.finish(total)
+            self.full[pl.ds(self.row(0), rows), :] = self.finish(total)
             if self.direct:
                 self.start("go")
             self.start("gr", "gl", "gp")
@@ -174,7 +170,7 @@
             self.copy(kind).wait_send()
 
 
-def kernel(cfg, theta_hbm, lam_ref, mu_ref, ut_ref, a_hbm, y_ref, out_hbm, th, tb, av, sa, sb, kb, kv,
+def kernel(cfg, theta_hbm, lam_ref, mu_ref, ut_ref, a_hbm, y_ref, th_out, sb_out, kb_out, kv_out, th, tb, av, sa, sb, kb, kv,
            load_sem, store_sem, *chunk_bufs):
     chips, band, step, lik = cfg
     n_part, dim = th.shape
@@ -184,11 +180,15 @@
     own = nb // owners
     wide, sub = dim // 2, 512
     rank = ut_ref.shape[0]
-    pack = LANES // rank
     pull = 2.0 / band
     gain = step / n_part
     me = lax.axis_index("feat")
-    where = (lax.rem(me, CORES), me // CORES, chips)
+    core, chip = lax.rem(me, CORES), me // CORES
+    group = lax.axis_index("ens") * owners
+    chip_of = {hop: lax.rem(chip + hop + chips, chips) for hop in (-1, 0, 1, 2)}
+    ids = {hop: group + chip_of[hop] * CORES + core for hop in (-1, 1, 2)}
+    ids["pair"] = group + chip * CORES + (1 - core)
+    where = (core, chip, chips, chip_of, ids)
 
     def finish(name):
         if name[0] == "g":
@@ -217,13 +217,10 @@
     load_a(1).start()
     load_theta(1).start()
 
-    any_chunk = ch[CHUNKS[0]]
     barrier = pltpu.get_barrier_semaphore()
-    peers = [where[1] * CORES + (1 - where[0])]
-    peers += [any_chunk.chip_at(hop) * CORES + where[0] for hop in (1, -1, 2)]
-    for peer in peers:
-        pl.semaphore_signal(barrier, inc=1, device_id={"feat": peer}, device_id_type=MESH)
-    pl.semaphore_wait(barrier, len(peers))
+    for peer in ids.values():
+        pl.semaphore_signal(barrier, inc=1, device_id=peer, device_id_type=LOGICAL)
+    pl.semaphore_wait(barrier, len(ids))
 
     def columns(lo, hi):
         return [slice(n, n + sub) for n in range(lo, hi, sub)]
@@ -236,15 +233,15 @@
             n = pl.ds(pl.multiple_of(t * wide, wide), wide)
             tb[rows(i), n] = th[rows(i), n].astype(BF16)
 
-    def project(i):
-        q = jnp.zeros((nb, rank), F32)
+    def project():
+        q = jnp.zeros((rank, n_part), F32)
         for n in columns(0, dim):
-            q = q + dot((th[rows(i), n] - mu_ref[:, n]).astype(BF16), ut_ref[:, n], NT)
-        piece = 2 * own + 8
+            q = q + dot(ut_ref[:, n], (th[:, n] - mu_ref[:, n]).astype(BF16), NT)
+        piece, part = 2 * own + 8, rank // owners
         for o in range(owners):
-            parts = [q[o * own + 8 * k:o * own + 8 * (k + 1)] for k in range(pack)]
-            ch["g1"].part[o * piece + 2 * own:(o + 1) * piece, i * LANES:(i + 1) * LANES] = \
-                jnp.concatenate(parts, axis=1)
+            for i in range(2):
+                lo = o * piece + 2 * own + i * part
+                ch["g1"].part[lo:lo + part, :] = q[o * part:(o + 1) * part, rows(i)]
 
     def gram(i):
         g = dot(tb[rows(i), :], tb[0:(i + 1) * nb, :], NT)
@@ -258,16 +255,13 @@
         ch[name].part[...] = dot(tb[rows(i), :], av[j * mc:(j + 1) * mc, :], NT)
 
     def base(i, n, q):
-        t = th[rows(i), n]
-        return -((t - mu_ref[:, n]) * lam_ref[:, n]) - dot(q, ut_ref[:, n]) - pull * tb[rows(i), n].astype(F32)
+        x = th[rows(i), n] - mu_ref[:, n]
+        return x * lam_ref[:, n] + dot(q, ut_ref[:, n]) + pull * tb[rows(i), n].astype(F32)
 
     def gathered_q(i):
-        piece = 2 * own + 8
-        parts = []
-        for o in range(owners):
-            p = ch["g1"].full[o * piece + 2 * own:(o + 1) * piece, i * LANES:(i + 1) * LANES]
-            parts += [p[:, rank * k:rank * (k + 1)] for k in range(pack)]
-        return jnp.concatenate(parts, axis=0).astype(BF16)
+        piece, part = 2 * own + 8, rank // owners
+        los = [o * piece + 2 * own + i * part for o in range(owners)]
+        return jnp.concatenate([ch["g1"].full[lo:lo + part, :] for lo in los], axis=0).T.astype(BF16)
 
     def both_lik(lo, hi):
         for n in columns(lo, hi):
@@ -284,7 +278,7 @@
     def low_rank(i):
         q = gathered_q(i)
         for n in columns(0, dim):
-            s = sa[rows(i), n] + base(i, n, q)
+            s = sa[rows(i), n] - base(i, n, q)
             if i == 0:
                 sb[rows(i), n] = s.astype(BF16)
             else:
@@ -315,22 +309,24 @@
             total = jnp.sum(pair[0], axis=1, keepdims=True) + jnp.sum(pair[1], axis=1, keepdims=True)
             kv[rows(i), :] = jnp.broadcast_to(gain * pull * total, (nb, LANES))
 
-    def drive(i, lo, hi, out=False):
+    def drive(i, lo, hi):
         for n in columns(lo, hi):
             t = th[rows(i), n]
             scale = jnp.concatenate([kv[rows(i), :]] * (sub // LANES), axis=1)
             t = t + (scale * t + gain * dot(kb[rows(i), :], sb[:, n]))
             th[rows(i), n] = t
-            if not out:
-                tb[rows(i), n] = t.astype(BF16)
-
-    def store(i, lo, hi):
-        n = pl.ds(lo, hi - lo)
-        return pltpu.make_async_copy(th.at[rows(i), n], out_hbm.at[rows(i), n], store_sem.at[2 * i + lo // (hi - lo)])
+            tb[rows(i), n] = t.astype(BF16)
+
+    outs = dict(th0=(th, th_out, rows(0)), th1=(th, th_out, rows(1)), sb0=(sb, sb_out, rows(0)),
+                sb1=(sb, sb_out, rows(1)), kb=(kb, kb_out, slice(0, n_part)), kv=(kv, kv_out, slice(0, n_part)))
+    out_copies = {}
+    for k, (name, (src, dst, r)) in enumerate(outs.items()):
+        out_copies[name] = pltpu.make_async_copy(src.at[r, :], dst.at[r, :], store_sem.at[k])
+    ready = {"drive1b": ("th0", "th1"), "lr0": ("sb0",), "ll1b": ("sb1",), "kmat": ("kb", "kv")}
 
     halves = {"a": (0, wide), "b": (wide, dim)}
     pieces = {
-        "proj0": lambda: project(0), "proj1": lambda: project(1), "gram0": lambda: gram(0), "gram1": lambda: gram(1),
+        "proj": project, "gram0": lambda: gram(0), "gram1": lambda: gram(1),
         "z0p": lambda: logit("z0", 0, 0), "z0q": lambda: logit("z3", 0, 1),
         "z1": lambda: logit("z1", 1, 0), "z2": lambda: logit("z2", 1, 1),
         "lr0": lambda: low_rank(0), "lr1": lambda: low_rank(1), "kmat": kernel_mat,
@@ -368,16 +364,22 @@
                 pl.when(s < NUM_STEPS - 1)(pieces[item])
             else:
                 pieces[item]()
+            if item in ready:
+                @pl.when(s == NUM_STEPS - 1)
+                def _():
+                    for name in ready[item]:
+                        out_copies[name].start()
         for name in CHUNKS:
             ch[name].drain()
 
-    for i in range(2):
-        for lo, hi in halves.values():
-            drive(i, lo, hi, out=True)
-            store(i, lo, hi).start()
-    for i in range(2):
-        for lo, hi in halves.values():
-            store(i, lo, hi).wait()
+    for copy in out_copies.values():
+        copy.wait()
+
+
+def last_drive(gain, th_ref, sb_ref, kb_ref, kv_ref, out_ref):
+    t = th_ref[...]
+    scale = jnp.concatenate([kv_ref[...]] * (t.shape[1] // LANES), axis=1)
+    out_ref[...] = t + (scale * t + gain * dot(kb_ref[...], sb_ref[...]))
 
 
 def solution(mesh):
@@ -396,7 +398,7 @@
         scratch = [
             pltpu.VMEM((n_part, dim), F32), pltpu.VMEM((n_part, dim), BF16), pltpu.VMEM((m_rows, dim), BF16),
             pltpu.VMEM((n_part, dim), F32), pltpu.VMEM((n_part, dim), BF16),
-            pltpu.VMEM((n_part, n_part), BF16), pltpu.VMEM((n_part, LANES), F32), dma((4,)), dma((4,)),
+            pltpu.VMEM((n_part, n_part), BF16), pltpu.VMEM((n_part, LANES), F32), dma((4,)), dma((6,)),
         ]
         for name in CHUNKS:
             wire, width, rows = (F32, nb, own) if name[0] == "g" else (BF16, mc, own)
@@ -408,16 +410,28 @@
                 pltpu.VMEM((3 * rows, width), wire), pltpu.VMEM((3 * rows, width), wire),
                 pltpu.VMEM((feat_size * rows, width), wire), dma((count,)), dma((count,)),
             ]
-        return pl.pallas_call(
+        outs = [((n_part, dim), F32), ((n_part, dim), BF16), ((n_part, n_part), BF16), ((n_part, LANES), F32)]
+        th, sb, kb, kv = pl.pallas_call(
             functools.partial(kernel, cfg),
-            out_shape=jax.ShapeDtypeStruct((n_part, dim), F32),
+            out_shape=[jax.ShapeDtypeStruct(*o) for o in outs],
             in_specs=[any_, vm, vm, vm, any_, vm],
-            out_specs=any_,
+            out_specs=[any_] * 4,
             scratch_shapes=scratch,
             compiler_params=pltpu.CompilerParams(
                 collective_id=0, has_side_effects=True, vmem_limit_bytes=60 * 2**20),
             cost_estimate=pl.CostEstimate(flops=60 * 10**9, bytes_accessed=32 * 2**20, transcendentals=0),
         )(particles, prec_diag[None, :], prior_mean[None, :], low_factor.T, data_mat, labels[None, :])
+        width = 512
+        by_column = pl.BlockSpec((n_part, width), lambda n: (0, n))
+        whole = lambda x: pl.BlockSpec(x.shape, lambda n: (0, 0))
+        return pl.pallas_call(
+            functools.partial(last_drive, dim_full / 4.0 / n_part),
+            out_shape=jax.ShapeDtypeStruct((n_part, dim), F32),
+            grid=(dim // width,),
+            in_specs=[by_column, by_column, whole(kb), whole(kv)],
+            out_specs=by_column,
+            cost_estimate=pl.CostEstimate(flops=2 * n_part * n_part * dim, bytes_accessed=20 * 2**20, transcendentals=0),
+        )(th, sb, kb, kv)
 
     return jax.shard_map(
         local_run,

time: 119 us -> 116 us (0.975)
  local copies, waits for them, and re-layouts: 7.77 us -> 0 us
  Pallas kernels: 111 us -> 115 us
    unnamed x1 -> x0, local copies, waits for them, and re-layouts: 7.77 us -> none
    pallas_call x1 -> x2, Pallas kernels: 111 us -> 115 us  [the longest x1 104 us: local_run(): pl.pallas_call(functools.partial(kernel, cfg), out_shape=[jax.ShapeDtypeS...]
where the time goes in v3:
time: 116 us; the launch traced here: 115 us
  Pallas kernels  115 us (99%)
    pallas_call x1, Pallas kernels, local_run(): pl.pallas_call(functools.partial(kernel, cfg), out_shape=[jax.ShapeDtypeS...  104 us
    pallas_call x1, Pallas kernels, local_run(): pl.pallas_call(functools.partial(last_drive, dim_full / 4.0 / n_part), ou...  11.3 us

profile of v3, /device:TPU:113, one launch (start us, length us, event | category | flops | bytes accessed | tf_op | source)
XLA Modules:
  0.0 115.3 jit_solution(16458851279358210442)
XLA Ops:
  0.0 104.0 %shard_map.64 = (f32[512,4096]{1,0:T(8,128)}, bf16[512,4096]{1,0:T(8,128)(2,1)}, bf16[512,512]{1,0:T(8,128)(2,1)}, f32[512,128]{1,0:T(8,128)}) custom-call(f32[512,4096]{1,0:T(8,128)} %theta_hbm.1, f32[1,4096]{1,0:T(1,128)} %bitcast.5, f32[1,4096]{1,0:T(1,128)} %bitcast.6, bf16[32,4096]{1,0:T(8,128)(2,1)} %bitcast.4, bf16[1024,4096]{1,0:T(8,128)(2,1)} %a_hbm.1, ...), custom_call_target="tpu_custom_call" | custom-call | flops 60000002048 | bytes 33554432 | tf_op jit(solution)/shard_map/pallas_call | solution.py:414
  104.0 11.3 %shard_map.65 = f32[512,4096]{1,0:T(8,128)} custom-call(f32[512,4096]{1,0:T(8,128)} %get-tuple-element.9.th_ref, bf16[512,4096]{1,0:T(8,128)(2,1)} %get-tuple-element.10.sb_ref, bf16[512,512]{1,0:T(8,128)(2,1)} %get-tuple-element.11.kb_ref, f32[512,128]{1,0:T(8,128)} %get-tuple-element.12.kv_ref), custom_call_target="tpu_custom_call" | custom-call | flops 2147483648 | bytes 20971520 | tf_op jit(solution)/shard_map/pallas_call | solution.py:427

commit v4 on v3

--- a/solution.py
+++ b/solution.py
@@ -170,8 +170,8 @@
             self.copy(kind).wait_send()
 
 
-def kernel(cfg, theta_hbm, lam_ref, mu_ref, ut_ref, a_hbm, y_ref, th_out, sb_out, kb_out, kv_out, th, tb, av, sa, sb, kb, kv,
-           load_sem, store_sem, *chunk_bufs):
+def kernel(cfg, theta_hbm, lam_ref, mu_ref, ut_ref, a_hbm, y_ref, th, tb, av, sa, sb, kb, kv,
+           load_sem, *chunk_bufs):
     chips, band, step, lik = cfg
     n_part, dim = th.shape
     m_rows = av.shape[0]
@@ -317,13 +317,6 @@
             th[rows(i), n] = t
             tb[rows(i), n] = t.astype(BF16)
 
-    outs = dict(th0=(th, th_out, rows(0)), th1=(th, th_out, rows(1)), sb0=(sb, sb_out, rows(0)),
-                sb1=(sb, sb_out, rows(1)), kb=(kb, kb_out, slice(0, n_part)), kv=(kv, kv_out, slice(0, n_part)))
-    out_copies = {}
-    for k, (name, (src, dst, r)) in enumerate(outs.items()):
-        out_copies[name] = pltpu.make_async_copy(src.at[r, :], dst.at[r, :], store_sem.at[k])
-    ready = {"drive1b": ("th0", "th1"), "lr0": ("sb0",), "ll1b": ("sb1",), "kmat": ("kb", "kv")}
-
     halves = {"a": (0, wide), "b": (wide, dim)}
     pieces = {
         "proj": project, "gram0": lambda: gram(0), "gram1": lambda: gram(1),
@@ -360,26 +353,13 @@
                     prep(1)
             if item[:6] == "drive1":
                 pl.when(s > 0)(pieces[item])
-            elif item[:6] == "drive0":
-                pl.when(s < NUM_STEPS - 1)(pieces[item])
             else:
                 pieces[item]()
-            if item in ready:
-                @pl.when(s == NUM_STEPS - 1)
-                def _():
-                    for name in ready[item]:
-                        out_copies[name].start()
         for name in CHUNKS:
             ch[name].drain()
 
-    for copy in out_copies.values():
-        copy.wait()
-
-
-def last_drive(gain, th_ref, sb_ref, kb_ref, kv_ref, out_ref):
-    t = th_ref[...]
-    scale = jnp.concatenate([kv_ref[...]] * (t.shape[1] // LANES), axis=1)
-    out_ref[...] = t + (scale * t + gain * dot(kb_ref[...], sb_ref[...]))
+    for lo, hi in halves.values():
+        drive(1, lo, hi)
 
 
 def solution(mesh):
@@ -396,9 +376,9 @@
         vm, any_ = pl.BlockSpec(memory_space=pltpu.VMEM), pl.BlockSpec(memory_space=pl.ANY)
         dma = pltpu.SemaphoreType.DMA
         scratch = [
-            pltpu.VMEM((n_part, dim), F32), pltpu.VMEM((n_part, dim), BF16), pltpu.VMEM((m_rows, dim), BF16),
+            pltpu.VMEM((n_part, dim), BF16), pltpu.VMEM((m_rows, dim), BF16),
             pltpu.VMEM((n_part, dim), F32), pltpu.VMEM((n_part, dim), BF16),
-            pltpu.VMEM((n_part, n_part), BF16), pltpu.VMEM((n_part, LANES), F32), dma((4,)), dma((6,)),
+            pltpu.VMEM((n_part, n_part), BF16), pltpu.VMEM((n_part, LANES), F32), dma((4,)),
         ]
         for name in CHUNKS:
             wire, width, rows = (F32, nb, own) if name[0] == "g" else (BF16, mc, own)
@@ -410,28 +390,16 @@
                 pltpu.VMEM((3 * rows, width), wire), pltpu.VMEM((3 * rows, width), wire),
                 pltpu.VMEM((feat_size * rows, width), wire), dma((count,)), dma((count,)),
             ]
-        outs = [((n_part, dim), F32), ((n_part, dim), BF16), ((n_part, n_part), BF16), ((n_part, LANES), F32)]
-        th, sb, kb, kv = pl.pallas_call(
+        return pl.pallas_call(
             functools.partial(kernel, cfg),
-            out_shape=[jax.ShapeDtypeStruct(*o) for o in outs],
+            out_shape=pltpu.VMEM((n_part, dim), F32),
             in_specs=[any_, vm, vm, vm, any_, vm],
-            out_specs=[any_] * 4,
+            out_specs=vm,
             scratch_shapes=scratch,
             compiler_params=pltpu.CompilerParams(
-                collective_id=0, has_side_effects=True, vmem_limit_bytes=60 * 2**20),
+                collective_id=0, has_side_effects=True, vmem_limit_bytes=48 * 2**20),
             cost_estimate=pl.CostEstimate(flops=60 * 10**9, bytes_accessed=32 * 2**20, transcendentals=0),
         )(particles, prec_diag[None, :], prior_mean[None, :], low_factor.T, data_mat, labels[None, :])
-        width = 512
-        by_column = pl.BlockSpec((n_part, width), lambda n: (0, n))
-        whole = lambda x: pl.BlockSpec(x.shape, lambda n: (0, 0))
-        return pl.pallas_call(
-            functools.partial(last_drive, dim_full / 4.0 / n_part),
-            out_shape=jax.ShapeDtypeStruct((n_part, dim), F32),
-            grid=(dim // width,),
-            in_specs=[by_column, by_column, whole(kb), whole(kv)],
-            out_specs=by_column,
-            cost_estimate=pl.CostEstimate(flops=2 * n_part * n_part * dim, bytes_accessed=20 * 2**20, transcendentals=0),
-        )(th, sb, kb, kv)
 
     return jax.shard_map(
         local_run,

time: 116 us -> 109 us (0.940)
  Pallas kernels: 115 us -> 105 us
  local copies, waits for them, and re-layouts: 0 us -> 3.4 us
    pallas_call x2 -> x1, Pallas kernels: 115 us -> 105 us  [local_run(): pl.pallas_call(functools.partial(kernel, cfg), out_shape=pltpu.VMEM((n_pa...]
    unnamed x0 -> x1, local copies, waits for them, and re-layouts: none -> 3.4 us
where the time goes in v4:
time: 109 us
  Pallas kernels  105 us (96%)
  local copies, waits for them, and re-layouts  3.4 us (3%)
    pallas_call x1, Pallas kernels, local_run(): pl.pallas_call(functools.partial(kernel, cfg), out_shape=pltpu.VMEM((n_pa...  105 us
    unnamed x1, local copies, waits for them, and re-layouts  3.4 us

profile of v4, /device:TPU:113, one launch (start us, length us, event | category | flops | bytes accessed | tf_op | source)
XLA Modules:
  0.0 108.9 jit_solution(14725074327377606842)
XLA Ops:
  0.0 105.4 %shard_map.64 = f32[512,4096]{1,0:T(8,128)S(1)} custom-call(f32[512,4096]{1,0:T(8,128)} %theta_hbm.1, f32[1,4096]{1,0:T(1,128)} %bitcast.5, f32[1,4096]{1,0:T(1,128)} %bitcast.6, bf16[32,4096]{1,0:T(8,128)(2,1)} %bitcast.4, bf16[1024,4096]{1,0:T(8,128)(2,1)} %a_hbm.1, s32[1,1024]{1,0:T(1,128)} %bitcast.7), custom_call_target="tpu_custom_call" | custom-call | flops 60000002048 | bytes 33554432 | tf_op jit(solution)/shard_map/pallas_call | solution.py:393
  105.5 3.4 %copy.8 = f32[512,4096]{1,0:T(8,128)} copy(f32[512,4096]{1,0:T(8,128)S(1)} %shard_map.64) | data formatting | bytes 16777216

commit v5 on v4

--- a/solution.py
+++ b/solution.py
@@ -18,13 +18,13 @@
          "gr", "gl", "gp", "fa", "flp", "fb", "frp", "fop")
 DIRECT_KINDS = ("d2d", "ir", "il", "io", "gr", "gl", "go", "gp", "flp", "frp", "fop")
 CHUNKS = ("g0", "z0", "z3", "g1", "z1", "z2")
-DIRECT = ('g0', 'g1', 'z0', 'z1', 'z2', 'z3')
+DIRECT = ('z0', 'z3', 'z1', 'z2', 'g0', 'g1')
 SCHEDULE = (
-    "z0q", "z3:0", "z0p", "z0:0", "z3:1", "gram0", "z0:1", "g0:0", "drive1a", "drive1b", "g0:1", "z1",
-    "z3:3", "z1:0", "gram1", "z0:3", "proj", "g1:0", "z1:1", "g1:1", "z3:4", "z3:5", "z2", "z0:4",
-    "z1:3", "z0:5", "z2:0", "z2:1", "z3:6", "g1:3", "z0:6", "z1:4", "l0a", "z2:3", "g0:3", "z1:5",
-    "l0b", "z1:6", "lf1a", "lf1b", "g1:4", "g1:5", "z2:4", "z2:5", "g1:6", "lr1", "z2:6", "ll1a",
-    "g0:4", "g0:5", "ll1b", "lr0", "g0:6", "kmat", "drive0a", "drive0b",
+    "gram0", "g0:0", "z0p", "z0:0", "drive1a", "g0:1", "z0q", "z3:0", "drive1b", "z0:1", "z1", "z1:0",
+    "z3:1", "proj", "z1:1", "gram1", "z0:3", "g1:0", "z3:3", "z2", "z2:0", "g1:1", "z1:3", "z2:1",
+    "z3:4", "z3:5", "z0:4", "z0:5", "g1:3", "z1:4", "z3:6", "z0:6", "z1:5", "l0a", "g0:3", "z1:6",
+    "z2:3", "lf1a", "lf1b", "l0b", "g1:4", "g1:5", "g0:4", "g0:5", "g1:6", "lr0", "z2:4", "z2:5",
+    "lr1", "g0:6", "kmat", "z2:6", "ll1a", "d1", "d0", "ll1b", "drive0a", "drive0b",
 )
 
 
@@ -179,6 +179,10 @@
     owners = CORES * chips
     own = nb // owners
     wide, sub = dim // 2, 512
+    blocks = [[(a, b) for a in (2 * i, 2 * i + 1) for b in range(a + 1)] for i in range(2)]
+    share = LANES // owners
+    q_row = len(blocks[1]) * share
+    g1_piece = q_row + ut_ref.shape[0] // owners * (n_part // LANES)
     rank = ut_ref.shape[0]
     pull = 2.0 / band
     gain = step / n_part
@@ -237,19 +241,20 @@
         q = jnp.zeros((rank, n_part), F32)
         for n in columns(0, dim):
             q = q + dot(ut_ref[:, n], (th[:, n] - mu_ref[:, n]).astype(BF16), NT)
-        piece, part = 2 * own + 8, rank // owners
+        part = rank // owners
         for o in range(owners):
-            for i in range(2):
-                lo = o * piece + 2 * own + i * part
-                ch["g1"].part[lo:lo + part, :] = q[o * part:(o + 1) * part, rows(i)]
+            for k in range(n_part // LANES):
+                lo = o * g1_piece + q_row + k * part
+                ch["g1"].part[lo:lo + part, :] = q[o * part:(o + 1) * part, k * LANES:(k + 1) * LANES]
 
     def gram(i):
         g = dot(tb[rows(i), :], tb[0:(i + 1) * nb, :], NT)
         part = ch[f"g{i}"].part
         piece = part.shape[0] // owners
-        for j in range(i + 1):
+        for k, (a, b) in enumerate(blocks[i]):
+            block = g[(a - 2 * i) * LANES:(a - 2 * i + 1) * LANES, b * LANES:(b + 1) * LANES]
             for o in range(owners):
-                part[o * piece + j * own:o * piece + (j + 1) * own, :] = g[o * own:(o + 1) * own, j * nb:(j + 1) * nb]
+                part[o * piece + k * share:o * piece + (k + 1) * share, :] = block[o * share:(o + 1) * share]
 
     def logit(name, i, j):
         ch[name].part[...] = dot(tb[rows(i), :], av[j * mc:(j + 1) * mc, :], NT)
@@ -259,9 +264,12 @@
         return x * lam_ref[:, n] + dot(q, ut_ref[:, n]) + pull * tb[rows(i), n].astype(F32)
 
     def gathered_q(i):
-        piece, part = 2 * own + 8, rank // owners
-        los = [o * piece + 2 * own + i * part for o in range(owners)]
-        return jnp.concatenate([ch["g1"].full[lo:lo + part, :] for lo in los], axis=0).T.astype(BF16)
+        part = rank // owners
+        parts = []
+        for k in range(i * nb // LANES, (i + 1) * nb // LANES):
+            los = [o * g1_piece + q_row + k * part for o in range(owners)]
+            parts.append(jnp.concatenate([ch["g1"].full[lo:lo + part, :] for lo in los], axis=0).T)
+        return jnp.concatenate(parts, axis=0).astype(BF16)
 
     def both_lik(lo, hi):
         for n in columns(lo, hi):
@@ -285,35 +293,36 @@
                 sa[rows(i), n] = s
 
     def kernel_mat():
-        def block(name, j):
-            full = ch[name].full
+        grams = {}
+        for i in range(2):
+            full = ch[f"g{i}"].full
             piece = full.shape[0] // owners
-            return jnp.concatenate(
-                [full[o * piece + j * own:o * piece + (j + 1) * own, :] for o in range(owners)], axis=0)
-
-        def diag(g):
-            eye = lax.broadcasted_iota(jnp.int32, g.shape, 0) == lax.broadcasted_iota(jnp.int32, g.shape, 1)
-            d = jnp.where(eye, g, 0.0)
-            return jnp.sum(d, axis=1, keepdims=True), jnp.sum(d, axis=0, keepdims=True)
-
-        def rbf(c, r, g):
-            return jnp.exp(-jnp.maximum(c + r - 2.0 * g, 0.0) / band)
-
-        g00, g10, g11 = block("g0", 0), block("g1", 0), block("g1", 1)
-        (c0, r0), (c1, r1) = diag(g00), diag(g11)
-        k00, k10, k11 = rbf(c0, r0, g00), rbf(c1, r0, g10), rbf(c1, r1, g11)
-        k01 = k10.T
-        for i, j, k in ((0, 0, k00), (0, 1, k01), (1, 0, k10), (1, 1, k11)):
-            kb[rows(i), rows(j)] = k.astype(BF16)
-        for i, pair in ((0, (k00, k01)), (1, (k10, k11))):
-            total = jnp.sum(pair[0], axis=1, keepdims=True) + jnp.sum(pair[1], axis=1, keepdims=True)
-            kv[rows(i), :] = jnp.broadcast_to(gain * pull * total, (nb, LANES))
+            for k, ab in enumerate(blocks[i]):
+                grams[ab] = jnp.concatenate(
+                    [full[o * piece + k * share:o * piece + (k + 1) * share, :] for o in range(owners)], axis=0)
+        eye = lax.broadcasted_iota(jnp.int32, (LANES, LANES), 0) == lax.broadcasted_iota(jnp.int32, (LANES, LANES), 1)
+        count = n_part // LANES
+        norms = [jnp.where(eye, grams[a, a], 0.0) for a in range(count)]
+        cols = [jnp.sum(d, axis=1, keepdims=True) for d in norms]
+        lines = [jnp.sum(d, axis=0, keepdims=True) for d in norms]
+        totals = [0.0] * count
+        for (a, b), g in grams.items():
+            k = jnp.exp(-jnp.maximum(cols[a] + lines[b] - 2.0 * g, 0.0) / band)
+            for i, j, m in ((a, b, k), (b, a, k.T))[:2 if a != b else 1]:
+                kb[i * LANES:(i + 1) * LANES, j * LANES:(j + 1) * LANES] = m.astype(BF16)
+                totals[i] = totals[i] + jnp.sum(m, axis=1, keepdims=True)
+        for a in range(count):
+            kv[a * LANES:(a + 1) * LANES, :] = jnp.broadcast_to(gain * pull * totals[a], (LANES, LANES))
+
+    def drive_first(i):
+        for n in columns(0, dim):
+            t = th[rows(i), n]
+            scale = jnp.concatenate([kv[rows(i), :]] * (sub // LANES), axis=1)
+            th[rows(i), n] = t + (scale * t + gain * dot(kb[rows(i), rows(0)], sb[rows(0), n]))
 
     def drive(i, lo, hi):
         for n in columns(lo, hi):
-            t = th[rows(i), n]
-            scale = jnp.concatenate([kv[rows(i), :]] * (sub // LANES), axis=1)
-            t = t + (scale * t + gain * dot(kb[rows(i), :], sb[:, n]))
+            t = th[rows(i), n] + gain * dot(kb[rows(i), rows(1)], sb[rows(1), n])
             th[rows(i), n] = t
             tb[rows(i), n] = t.astype(BF16)
 
@@ -323,6 +332,7 @@
         "z0p": lambda: logit("z0", 0, 0), "z0q": lambda: logit("z3", 0, 1),
         "z1": lambda: logit("z1", 1, 0), "z2": lambda: logit("z2", 1, 1),
         "lr0": lambda: low_rank(0), "lr1": lambda: low_rank(1), "kmat": kernel_mat,
+        "d0": lambda: drive_first(0), "d1": lambda: drive_first(1),
     }
     for h, (lo, hi) in halves.items():
         pieces["l0" + h] = functools.partial(both_lik, lo, hi)
@@ -369,6 +379,7 @@
     def local_run(particles, prec_diag, low_factor, prior_mean, data_mat, labels):
         n_part, dim = particles.shape
         m_rows = data_mat.shape[0]
+        rank = low_factor.shape[1]
         dim_full = dim * feat_size
         cfg = (chips, 2.0 * dim_full, dim_full / 4.0, 2.0 / math.sqrt(m_rows * dim_full))
         nb, mc = n_part // 2, m_rows // 2
@@ -381,9 +392,9 @@
             pltpu.VMEM((n_part, n_part), BF16), pltpu.VMEM((n_part, LANES), F32), dma((4,)),
         ]
         for name in CHUNKS:
-            wire, width, rows = (F32, nb, own) if name[0] == "g" else (BF16, mc, own)
+            wire, width, rows = (F32, LANES, own // 2 * 3) if name[0] == "g" else (BF16, mc, own)
             if name == "g1":
-                rows = 2 * own + 8
+                rows = own // 2 * 7 + rank * n_part // LANES // feat_size
             count = len(DIRECT_KINDS if name in DIRECT else KINDS)
             scratch += [
                 pltpu.VMEM((feat_size * rows, width), F32), pltpu.VMEM((chips * rows, width), F32),

time: 109 us -> 106 us (0.972)
  Pallas kernels: 105 us -> 102 us
    pallas_call x1, Pallas kernels: 105 us -> 102 us  [local_run(): pl.pallas_call(functools.partial(kernel, cfg), out_shape=pltpu.VMEM((n_pa...]
where the time goes in v5:
time: 106 us
  Pallas kernels  102 us (96%)
  local copies, waits for them, and re-layouts  3.4 us (3%)
    pallas_call x1, Pallas kernels, local_run(): pl.pallas_call(functools.partial(kernel, cfg), out_shape=pltpu.VMEM((n_pa...  102 us
    unnamed x1, local copies, waits for them, and re-layouts  3.4 us

profile of v5, /device:TPU:113, one launch (start us, length us, event | category | flops | bytes accessed | tf_op | source)
XLA Modules:
  0.0 105.7 jit_solution(10778166833178887736)
XLA Ops:
  0.0 102.3 %shard_map.64 = f32[512,4096]{1,0:T(8,128)S(1)} custom-call(f32[512,4096]{1,0:T(8,128)} %theta_hbm.1, f32[1,4096]{1,0:T(1,128)} %bitcast.5, f32[1,4096]{1,0:T(1,128)} %bitcast.6, bf16[32,4096]{1,0:T(8,128)(2,1)} %bitcast.4, bf16[1024,4096]{1,0:T(8,128)(2,1)} %a_hbm.1, s32[1,1024]{1,0:T(1,128)} %bitcast.7), custom_call_target="tpu_custom_call" | custom-call | flops 60000002048 | bytes 33554432 | tf_op jit(solution)/shard_map/pallas_call | solution.py:404
  102.3 3.4 %copy.8 = f32[512,4096]{1,0:T(8,128)} copy(f32[512,4096]{1,0:T(8,128)S(1)} %shard_map.64) | data formatting | bytes 16777216

commit v6 on v5

--- a/solution.py
+++ b/solution.py
@@ -14,17 +14,17 @@
 NN = (((1,), (0,)), ((), ()))
 NT = (((1,), (1,)), ((), ()))
 LOGICAL = pl.DeviceIdType.LOGICAL
-KINDS = ("d2d", "s1a", "s1b", "ownb", "owna", "reda", "redb",
-         "gr", "gl", "gp", "fa", "flp", "fb", "frp", "fop")
-DIRECT_KINDS = ("d2d", "ir", "il", "io", "gr", "gl", "go", "gp", "flp", "frp", "fop")
+KINDS = ("d2d", "s1a", "s1b", "ownb", "owna", "reda", "redb", "ir", "il", "io",
+         "gr", "gl", "go", "gp", "fa", "flp", "fb", "frp", "fop")
 CHUNKS = ("g0", "z0", "z3", "g1", "z1", "z2")
 DIRECT = ('z0', 'z3', 'z1', 'z2', 'g0', 'g1')
+GATHER_DIRECT = ('z1', 'z2', 'g0')
 SCHEDULE = (
-    "gram0", "g0:0", "z0p", "z0:0", "drive1a", "g0:1", "z0q", "z3:0", "drive1b", "z0:1", "z1", "z1:0",
-    "z3:1", "proj", "z1:1", "gram1", "z0:3", "g1:0", "z3:3", "z2", "z2:0", "g1:1", "z1:3", "z2:1",
-    "z3:4", "z3:5", "z0:4", "z0:5", "g1:3", "z1:4", "z3:6", "z0:6", "z1:5", "l0a", "g0:3", "z1:6",
-    "z2:3", "lf1a", "lf1b", "l0b", "g1:4", "g1:5", "g0:4", "g0:5", "g1:6", "lr0", "z2:4", "z2:5",
-    "lr1", "g0:6", "kmat", "z2:6", "ll1a", "d1", "d0", "ll1b", "drive0a", "drive0b",
+    "z0p", "z0:0", "gram0", "g0:0", "z0q", "z3:0", "z0:1", "drive1a", "drive1b", "g0:1", "gram1",
+    "z3:1", "proj", "g1:0", "z0:3", "g1:1", "z1", "z1:0", "z3:3", "z0:4", "z2", "z1:1", "z2:0",
+    "g1:3", "z3:4", "z2:1", "z1:3", "z0:5", "g1:4", "z3:5", "z0:6", "g0:3", "z3:6", "l0a", "z2:3",
+    "z1:4", "z1:5", "l0b", "g1:5", "z1:6", "lf1a", "lf1b", "g0:4", "g0:5", "g1:6", "lr0", "lr1",
+    "z2:4", "z2:5", "g0:6", "kmat", "d1", "d0", "z2:6", "ll1a", "ll1b", "drive0a", "drive0b",
 )
 
 
@@ -37,9 +37,12 @@
         self.part, self.pair, self.send, self.recv, self.full, self.ssem, self.rsem = bufs
         self.core, self.chip, self.chips, self.chip_of, self.ids = where
         self.rows = self.full.shape[0] // (CORES * self.chips)
-        self.half = self.rows // 32 * 16
+        self.half = self.rows // 2 // 16 * 16
         self.direct = name in DIRECT
-        self.kinds = DIRECT_KINDS if self.direct else KINDS
+        self.gather_direct = name in GATHER_DIRECT
+        unused = {"s1a", "s1b", "ownb", "owna", "reda", "redb"} if self.direct else {"ir", "il", "io"}
+        unused |= {"fa", "fb"} if self.gather_direct else {"go"}
+        self.kinds = [kind for kind in KINDS if kind not in unused]
         self.finish = finish
 
     def row(self, hop):
@@ -84,7 +87,7 @@
                 "frp": lambda: (same(self.row(right), rows), pair),
                 "fop": lambda: (same(self.row(opp), rows), pair),
             }[kind]()
-        k = self.kinds.index(kind)
+        k = KINDS.index(kind)
         return pltpu.make_async_remote_copy(
             src_ref=src, dst_ref=dst, send_sem=self.ssem.at[k], recv_sem=self.rsem.at[k],
             device_id=dev, device_id_type=LOGICAL)
@@ -144,20 +147,20 @@
                 self.wait("ownb", "owna", "reda", "redb")
                 total = total + self.got(rows, 2 * rows) + self.got(2 * rows, 3 * rows)
             self.full[pl.ds(self.row(0), rows), :] = self.finish(total)
-            if self.direct:
+            if self.gather_direct:
                 self.start("go")
             self.start("gr", "gl", "gp")
         elif n == 4:
             self.wait("gr")
-            if not self.direct:
+            if not self.gather_direct:
                 self.start("fa")
             self.start("flp")
             self.wait("gl")
-            if not self.direct:
+            if not self.gather_direct:
                 self.start("fb")
             self.start("frp")
         elif n == 5:
-            if self.direct:
+            if self.gather_direct:
                 self.wait("go")
             else:
                 self.wait("fa", "fb")
@@ -170,8 +173,8 @@
             self.copy(kind).wait_send()
 
 
-def kernel(cfg, theta_hbm, lam_ref, mu_ref, ut_ref, a_hbm, y_ref, th, tb, av, sa, sb, kb, kv,
-           load_sem, *chunk_bufs):
+def kernel(cfg, theta_hbm, lam_hbm, mu_hbm, ut_hbm, a_hbm, y_hbm, th, tb, av, sa, sb, kb, kv,
+           lam_ref, mu_ref, ut_ref, y_ref, load_sem, small_sem, *chunk_bufs):
     chips, band, step, lik = cfg
     n_part, dim = th.shape
     m_rows = av.shape[0]
@@ -220,6 +223,10 @@
     load_a(0).start()
     load_a(1).start()
     load_theta(1).start()
+    small = [pltpu.make_async_copy(src, dst, small_sem.at[k]) for k, (src, dst) in enumerate(
+        ((lam_hbm, lam_ref), (mu_hbm, mu_ref), (ut_hbm, ut_ref), (y_hbm, y_ref)))]
+    for copy in small:
+        copy.start()
 
     barrier = pltpu.get_barrier_semaphore()
     for peer in ids.values():
@@ -345,6 +352,8 @@
     def _(s):
         @pl.when(s == 0)
         def _():
+            for copy in small:
+                copy.wait()
             prep(0)
 
         loaded = set()
@@ -389,22 +398,23 @@
         scratch = [
             pltpu.VMEM((n_part, dim), BF16), pltpu.VMEM((m_rows, dim), BF16),
             pltpu.VMEM((n_part, dim), F32), pltpu.VMEM((n_part, dim), BF16),
-            pltpu.VMEM((n_part, n_part), BF16), pltpu.VMEM((n_part, LANES), F32), dma((4,)),
+            pltpu.VMEM((n_part, n_part), BF16), pltpu.VMEM((n_part, LANES), F32),
+            pltpu.VMEM((1, dim), F32), pltpu.VMEM((1, dim), F32), pltpu.VMEM((rank, dim), BF16),
+            pltpu.VMEM((1, m_rows), jnp.int32), dma((4,)), dma((4,)),
         ]
         for name in CHUNKS:
             wire, width, rows = (F32, LANES, own // 2 * 3) if name[0] == "g" else (BF16, mc, own)
             if name == "g1":
                 rows = own // 2 * 7 + rank * n_part // LANES // feat_size
-            count = len(DIRECT_KINDS if name in DIRECT else KINDS)
             scratch += [
                 pltpu.VMEM((feat_size * rows, width), F32), pltpu.VMEM((chips * rows, width), F32),
                 pltpu.VMEM((3 * rows, width), wire), pltpu.VMEM((3 * rows, width), wire),
-                pltpu.VMEM((feat_size * rows, width), wire), dma((count,)), dma((count,)),
+                pltpu.VMEM((feat_size * rows, width), wire), dma((len(KINDS),)), dma((len(KINDS),)),
             ]
         return pl.pallas_call(
             functools.partial(kernel, cfg),
             out_shape=pltpu.VMEM((n_part, dim), F32),
-            in_specs=[any_, vm, vm, vm, any_, vm],
+            in_specs=[any_] * 6,
             out_specs=vm,
             scratch_shapes=scratch,
             compiler_params=pltpu.CompilerParams(

time: 106 us -> 113 us (1.066)
  Pallas kernels: 102 us -> 110 us
    pallas_call x1, Pallas kernels: 102 us -> 110 us  [local_run(): pl.pallas_call(functools.partial(kernel, cfg), out_shape=pltpu.VMEM((n_pa...]
where the time goes in v6:
time: 113 us
  Pallas kernels  110 us (97%)
  local copies, waits for them, and re-layouts  3.4 us (3%)
    pallas_call x1, Pallas kernels, local_run(): pl.pallas_call(functools.partial(kernel, cfg), out_shape=pltpu.VMEM((n_pa...  110 us
    unnamed x1, local copies, waits for them, and re-layouts  3.4 us

profile of v6, /device:TPU:113, one launch (start us, length us, event | category | flops | bytes accessed | tf_op | source)
XLA Modules:
  0.0 113.3 jit_solution(5830680405839143265)
XLA Ops:
  0.0 109.9 %shard_map.64 = f32[512,4096]{1,0:T(8,128)S(1)} custom-call(f32[512,4096]{1,0:T(8,128)} %theta_hbm.1, f32[1,4096]{1,0:T(1,128)} %bitcast.5, f32[1,4096]{1,0:T(1,128)} %bitcast.6, bf16[32,4096]{1,0:T(8,128)(2,1)} %bitcast.4, bf16[1024,4096]{1,0:T(8,128)(2,1)} %a_hbm.1, s32[1,1024]{1,0:T(1,128)} %bitcast.7), custom_call_target="tpu_custom_call" | custom-call | flops 60000002048 | bytes 33554432 | tf_op jit(solution)/shard_map/pallas_call | solution.py:414
  109.9 3.4 %copy.8 = f32[512,4096]{1,0:T(8,128)} copy(f32[512,4096]{1,0:T(8,128)S(1)} %shard_map.64) | data formatting | bytes 16777216

commit v7 on v6

--- a/solution.py
+++ b/solution.py
@@ -18,13 +18,13 @@
          "gr", "gl", "go", "gp", "fa", "flp", "fb", "frp", "fop")
 CHUNKS = ("g0", "z0", "z3", "g1", "z1", "z2")
 DIRECT = ('z0', 'z3', 'z1', 'z2', 'g0', 'g1')
-GATHER_DIRECT = ('z1', 'z2', 'g0')
+GATHER_DIRECT = ('z0', 'z3', 'z1', 'z2', 'g0', 'g1')
 SCHEDULE = (
-    "z0p", "z0:0", "gram0", "g0:0", "z0q", "z3:0", "z0:1", "drive1a", "drive1b", "g0:1", "gram1",
-    "z3:1", "proj", "g1:0", "z0:3", "g1:1", "z1", "z1:0", "z3:3", "z0:4", "z2", "z1:1", "z2:0",
-    "g1:3", "z3:4", "z2:1", "z1:3", "z0:5", "g1:4", "z3:5", "z0:6", "g0:3", "z3:6", "l0a", "z2:3",
-    "z1:4", "z1:5", "l0b", "g1:5", "z1:6", "lf1a", "lf1b", "g0:4", "g0:5", "g1:6", "lr0", "lr1",
-    "z2:4", "z2:5", "g0:6", "kmat", "d1", "d0", "z2:6", "ll1a", "ll1b", "drive0a", "drive0b",
+    "z0p", "z0:0", "drive1a", "z0q", "z3:0", "z0:1", "drive1b", "gram0", "g0:0", "z1", "z1:0", "z3:1",
+    "gram1", "g0:1", "z1:1", "proj", "g1:0", "z0:3", "g1:1", "z2", "z2:0", "z3:3", "z2:1", "g0:3",
+    "z1:3", "g1:3", "z0:4", "z0:5", "z3:4", "z3:5", "z3:6", "z0:6", "z2:3", "l0a", "g0:4", "g0:5",
+    "z1:4", "z1:5", "l0b", "z1:6", "lf1a", "g0:6", "g1:4", "g1:5", "lf1b", "z2:4", "z2:5", "g1:6",
+    "kmat", "lr0", "z2:6", "lr1", "d1", "d0", "ll1a", "ll1b", "drive0a", "drive0b",
 )
 
 

time: 113 us -> 113 us (level)
  no operation moved by 1% of the time
where the time goes in v7:
time: 113 us
  Pallas kernels  109 us (96%)
  local copies, waits for them, and re-layouts  3.4 us (3%)
    pallas_call x1, Pallas kernels, local_run(): pl.pallas_call(functools.partial(kernel, cfg), out_shape=pltpu.VMEM((n_pa...  109 us
    unnamed x1, local copies, waits for them, and re-layouts  3.4 us

profile of v7, /device:TPU:113, one launch (start us, length us, event | category | flops | bytes accessed | tf_op | source)
XLA Modules:
  0.0 112.5 jit_solution(12275100696524890398)
XLA Ops:
  0.0 109.1 %shard_map.64 = f32[512,4096]{1,0:T(8,128)S(1)} custom-call(f32[512,4096]{1,0:T(8,128)} %theta_hbm.1, f32[1,4096]{1,0:T(1,128)} %bitcast.5, f32[1,4096]{1,0:T(1,128)} %bitcast.6, bf16[32,4096]{1,0:T(8,128)(2,1)} %bitcast.4, bf16[1024,4096]{1,0:T(8,128)(2,1)} %a_hbm.1, s32[1,1024]{1,0:T(1,128)} %bitcast.7), custom_call_target="tpu_custom_call" | custom-call | flops 60000002048 | bytes 33554432 | tf_op jit(solution)/shard_map/pallas_call | solution.py:414
  109.1 3.4 %copy.8 = f32[512,4096]{1,0:T(8,128)} copy(f32[512,4096]{1,0:T(8,128)S(1)} %shard_map.64) | data formatting | bytes 16777216

commit v8 on v7

--- a/solution.py
+++ b/solution.py
@@ -372,6 +372,8 @@
                     prep(1)
             if item[:6] == "drive1":
                 pl.when(s > 0)(pieces[item])
+            elif item in ("proj", "gram0"):
+                pl.when(me >= 0)(pieces[item])
             else:
                 pieces[item]()
         for name in CHUNKS:

time: 113 us -> 112 us (level)
  no operation moved by 1% of the time
where the time goes in v8:
time: 112 us; the launch traced here: 111 us
  Pallas kernels  108 us (96%)
  local copies, waits for them, and re-layouts  3.4 us (3%)
    pallas_call x1, Pallas kernels, local_run(): pl.pallas_call(functools.partial(kernel, cfg), out_shape=pltpu.VMEM((n_pa...  108 us
    unnamed x1, local copies, waits for them, and re-layouts  3.4 us

profile of v8, /device:TPU:113, one launch (start us, length us, event | category | flops | bytes accessed | tf_op | source)
XLA Modules:
  0.0 111.4 jit_solution(12011121667847586107)
XLA Ops:
  0.0 108.0 %shard_map.64 = f32[512,4096]{1,0:T(8,128)S(1)} custom-call(f32[512,4096]{1,0:T(8,128)} %theta_hbm.1, f32[1,4096]{1,0:T(1,128)} %bitcast.5, f32[1,4096]{1,0:T(1,128)} %bitcast.6, bf16[32,4096]{1,0:T(8,128)(2,1)} %bitcast.4, bf16[1024,4096]{1,0:T(8,128)(2,1)} %a_hbm.1, s32[1,1024]{1,0:T(1,128)} %bitcast.7), custom_call_target="tpu_custom_call" | custom-call | flops 60000002048 | bytes 33554432 | tf_op jit(solution)/shard_map/pallas_call | solution.py:416
  108.0 3.4 %copy.8 = f32[512,4096]{1,0:T(8,128)} copy(f32[512,4096]{1,0:T(8,128)S(1)} %shard_map.64) | data formatting | bytes 16777216

commit v9 on v7

--- a/solution.py
+++ b/solution.py
@@ -20,11 +20,11 @@
 DIRECT = ('z0', 'z3', 'z1', 'z2', 'g0', 'g1')
 GATHER_DIRECT = ('z0', 'z3', 'z1', 'z2', 'g0', 'g1')
 SCHEDULE = (
-    "z0p", "z0:0", "drive1a", "z0q", "z3:0", "z0:1", "drive1b", "gram0", "g0:0", "z1", "z1:0", "z3:1",
-    "gram1", "g0:1", "z1:1", "proj", "g1:0", "z0:3", "g1:1", "z2", "z2:0", "z3:3", "z2:1", "g0:3",
-    "z1:3", "g1:3", "z0:4", "z0:5", "z3:4", "z3:5", "z3:6", "z0:6", "z2:3", "l0a", "g0:4", "g0:5",
-    "z1:4", "z1:5", "l0b", "z1:6", "lf1a", "g0:6", "g1:4", "g1:5", "lf1b", "z2:4", "z2:5", "g1:6",
-    "kmat", "lr0", "z2:6", "lr1", "d1", "d0", "ll1a", "ll1b", "drive0a", "drive0b",
+    "gram0", "g0:0", "z0p", "z0:0", "drive1a", "g0:1", "z0q", "z3:0", "drive1b", "z0:1", "z1", "z1:0",
+    "z3:1", "proj", "z1:1", "gram1", "z0:3", "g1:0", "z3:3", "z2", "z2:0", "g1:1", "z1:3", "z2:1",
+    "z3:4", "z3:5", "z0:4", "z0:5", "g1:3", "z1:4", "z3:6", "z0:6", "z1:5", "l0a", "g0:3", "z1:6",
+    "z2:3", "lf1a", "lf1b", "l0b", "g1:4", "g1:5", "g0:4", "g0:5", "g1:6", "lr0", "z2:4", "z2:5",
+    "lr1", "g0:6", "kmat", "z2:6", "ll1a", "d1", "d0", "ll1b", "drive0a", "drive0b",
 )
 
 

time: 113 us -> 109 us (0.965)
  Pallas kernels: 109 us -> 105 us
    pallas_call x1, Pallas kernels: 109 us -> 105 us  [local_run(): pl.pallas_call(functools.partial(kernel, cfg), out_shape=pltpu.VMEM((n_pa...]
where the time goes in v9:
time: 109 us
  Pallas kernels  105 us (96%)
  local copies, waits for them, and re-layouts  3.4 us (3%)
    pallas_call x1, Pallas kernels, local_run(): pl.pallas_call(functools.partial(kernel, cfg), out_shape=pltpu.VMEM((n_pa...  105 us
    unnamed x1, local copies, waits for them, and re-layouts  3.4 us

profile of v9, /device:TPU:113, one launch (start us, length us, event | category | flops | bytes accessed | tf_op | source)
XLA Modules:
  0.0 108.5 jit_solution(15198447985225474978)
XLA Ops:
  0.0 105.1 %shard_map.64 = f32[512,4096]{1,0:T(8,128)S(1)} custom-call(f32[512,4096]{1,0:T(8,128)} %theta_hbm.1, f32[1,4096]{1,0:T(1,128)} %bitcast.5, f32[1,4096]{1,0:T(1,128)} %bitcast.6, bf16[32,4096]{1,0:T(8,128)(2,1)} %bitcast.4, bf16[1024,4096]{1,0:T(8,128)(2,1)} %a_hbm.1, s32[1,1024]{1,0:T(1,128)} %bitcast.7), custom_call_target="tpu_custom_call" | custom-call | flops 60000002048 | bytes 33554432 | tf_op jit(solution)/shard_map/pallas_call | solution.py:414
  105.1 3.4 %copy.8 = f32[512,4096]{1,0:T(8,128)} copy(f32[512,4096]{1,0:T(8,128)S(1)} %shard_map.64) | data formatting | bytes 16777216
